TPU v7x, 32 devices: a whole 2x2x4 slice. The times are simulated.
32 devices in a mesh: group: 4 (over y, core), row: 2 (over x), col: 4 (over z).
Axes of the slice: x: 2, y: 2, z: 4, core: 2. Of those that a mesh axis runs over, the one named last changes fastest.
Arguments:
- fronts: bfloat16 [8, 12288, 12288], P('group', 'row', 'col'), may hold values from -0.0546875 to 0.0546875
- samples: bfloat16 [256, 8, 12288], P('row', 'group', 'col'), may hold values from -6 to 6
- second_samples: bfloat16 [256, 8, 12288], P('col', 'group', 'row'), may hold values from -6 to 6
- front_sizes: int32 [8], replicated, may hold values from 1536 to 12288, as said below
- parent_ids: int32 [8], replicated, may hold values from 1 to 8, as said below
- block_maps: int32 [8, 2], replicated, may hold values from 0 to 2, as said below
Outputs:
- sampled: bfloat16 [256, 8, 12288], P('col', 'group', 'row')
- projected: bfloat16 [256, 8, 12288], P('row', 'group', 'col')
Inputs may be any that keep to these rules, and one draw needn't show every extreme that they name: `front_sizes`: every front has at least 1536 rows and some front has exactly 12288. `parent_ids`: a front's parent has a larger index; 8 marks a root; the last front is a root. `block_maps`: for a front f with a parent p, entry b with b * 6144 < front_sizes[f] names a parent block q with q * 6144 < front_sizes[p]; all other entries are 2; several child blocks may name one parent block.
All inputs are finite; a program needn't handle non-finite values.
Results may differ from a plain program's by a relative error of at most 0.009.
Values may be sent and summed in bfloat16 or wider, within the bound.
A program may use at most 192 MiB of HBM per device.

v0:
```python
import jax
import jax.numpy as jnp
from jax import lax
from jax.sharding import PartitionSpec as P


def swap_pairs(count):
    return [(0, 1), (1, 0)] if count == 2 else None


def gather_row(value, count, own_row, axis):
    if count != 2:
        return lax.all_gather(value, "row", axis=axis, tiled=True)
    other = lax.ppermute(value, "row", swap_pairs(count))
    first = own_row == 0
    return jnp.concatenate(
        [jnp.where(first, value, other), jnp.where(first, other, value)], axis=axis
    )


def scatter_row(value, count, own_row):
    if count != 2:
        return lax.psum_scatter(
            value.astype(jnp.bfloat16), "row", scatter_dimension=0, tiled=True
        ).astype(jnp.float32)
    half = value.shape[0] // 2
    kept = lax.dynamic_slice_in_dim(value, own_row * half, half, 0)
    sent = lax.dynamic_slice_in_dim(value, (1 - own_row) * half, half, 0).astype(jnp.bfloat16)
    return kept + lax.ppermute(sent, "row", swap_pairs(count)).astype(jnp.float32)


def shards(fronts, samples, second_samples, front_sizes, parent_ids, block_maps):
    local_count, tile_rows, tile_cols = fronts.shape
    row_count = lax.axis_size("row")
    own_group = lax.axis_index("group")
    own_row = lax.axis_index("row")
    own_col = lax.axis_index("col")
    total_fronts = parent_ids.shape[0]
    block_count = block_maps.shape[1]
    own_sizes = lax.dynamic_slice_in_dim(front_sizes, own_group * local_count, local_count, 0)
    row_keep = (own_row * tile_rows + jnp.arange(tile_rows, dtype=jnp.int32))[None, :] < own_sizes[
        :, None
    ]
    col_keep = (own_col * tile_cols + jnp.arange(tile_cols, dtype=jnp.int32))[None, :] < own_sizes[
        :, None
    ]
    own_fronts = own_group * local_count + jnp.arange(local_count, dtype=jnp.int32)
    masked = gather_row(samples, row_count, own_row, 0) * col_keep[None].astype(jnp.bfloat16)
    partial_value = jnp.einsum("sfk,fmk->sfm", masked, fronts, preferred_element_type=jnp.float32)
    partial_value = (partial_value * row_keep[None].astype(jnp.float32)).astype(jnp.bfloat16)
    sampled = lax.psum_scatter(partial_value, "col", scatter_dimension=0, tiled=True)
    portion = lax.all_gather(sampled, ("group", "row"), axis=1, tiled=True)
    number = portion.shape[1]
    source = jnp.arange(number, dtype=jnp.int32)
    front_index = source // (local_count * row_count) * local_count + source % local_count
    block_index = source // local_count % row_count
    front_hot = (front_index[:, None] == jnp.arange(total_fronts, dtype=jnp.int32)[None, :]).astype(
        jnp.int32
    )
    parent = jnp.sum(front_hot * parent_ids[None, :], axis=1)
    map_rows = jnp.sum(front_hot[:, :, None] * block_maps[None, :, :], axis=1)
    block_hot = (jnp.arange(block_count, dtype=jnp.int32)[None, :] == block_index[:, None]).astype(
        jnp.int32
    )
    target = jnp.sum(block_hot * map_rows, axis=1)
    weight = (parent[:, None] == own_fronts[None, :]) & (target[:, None] == own_row)
    extension = jnp.einsum(
        "sik,ij->sjk", portion, weight.astype(jnp.bfloat16), preferred_element_type=jnp.float32
    )
    combined = (second_samples.astype(jnp.float32) + extension).astype(jnp.bfloat16)
    combined = combined * row_keep[None].astype(jnp.bfloat16)
    gathered = lax.all_gather(combined, "col", axis=0, tiled=True)
    product = jnp.einsum("sfm,fmk->sfk", gathered, fronts, preferred_element_type=jnp.float32)
    projected = scatter_row(product, row_count, own_row)
    projected = (projected * col_keep[None].astype(jnp.float32)).astype(jnp.bfloat16)
    return (sampled, projected)


def solution(mesh):
    placed = (
        P("group", "row", "col"),
        P("row", "group", "col"),
        P("col", "group", "row"),
        P(),
        P(),
        P(),
    )
    return jax.shard_map(
        shards,
        mesh=mesh,
        in_specs=placed,
        out_specs=(P("col", "group", "row"), P("row", "group", "col")),
        check_vma=False,
    )
```

profile of v0, /device:TPU:0, one launch (start us, length us, event | category | flops | bytes accessed | tf_op | source)
XLA Modules:
  0.0 491.0 jit_solution(10001149116295977696)
XLA Ops:
  7.2 0.0 reduce-scatter.2.cloned.1.call-start
  7.2 3.0 collective-permute-start
  10.2 0.7 dynamic_slice.9
  11.0 0.1 compare_convert_fusion.2
  11.1 0.1 compare_convert_fusion
  11.2 33.7 %collective-permute-done = bf16[128,2,3072]{2,1,0:T(2,128)(2,1)S(1)} collective-permute-done((bf16[128,2,3072]{2,1,0:T(2,128)(2,1)}, bf16[128,2,3072]{2,1,0:T(2,128)(2,1)S(1)}, u32[]{:S(2)}, u32[]{:S(2)}) %collective-permute-start) | collective-permute-done | bytes 1572896 | tf_op jit(solution)/shard_map/ppermute | solution.py:14
  44.8 1.6 broadcast_select_fusion.1
  46.5 4.6 maximum_multiply_fusion
  51.0 32.3 %fusion.2 = bf16[256,2,6144]{2,0,1:T(8,128)(2,1)} fusion(bf16[2,6144,3072]{2,1,0:T(8,128)(2,1)} %param.6, f32[2,6144]{1,0:T(2,128)S(1)} %get-tuple-element.13, bf16[256,2,3072]{2,1,0:T(2,128)(2,1)S(1)} %maximum_multiply_fusion), kind=kOutput, calls=%fused_computation.3 | convolution fusion | flops 19333644288 | bytes 84983808 | tf_op jit(solution)/shard_map/sfk,fmk->sfm/dot_general | solution.py:49
  83.4 0.0 copy-start.1
  83.4 0.0 copy-start.3
  83.4 0.0 copy-start.2
  83.4 0.0 reduce-scatter.2.cloned.1.call-update
  83.4 0.0 all-gather.3.cloned.1.call-start
  83.5 112.4 %reduce-scatter.2.cloned.1.call-done = bf16[64,2,6144]{2,0,1:T(8,128)(2,1)} async-done(((bf16[256,2,6144]{2,0,1:T(8,128)(2,1)}), bf16[64,2,6144]{2,0,1:T(8,128)(2,1)}) %reduce-scatter.2.cloned.1.call-update) | async-done | bytes 1572880 | tf_op jit(solution)/shard_map/reduce_scatter | solution.py:51
  195.9 0.0 all-gather.3.cloned.1.call-update
  195.9 0.2 all-gather.5.cloned.1.call-start
  196.2 0.0 copy-done.1
  196.2 0.1 multiply_reduce_fusion
  196.3 0.0 copy-done.3
  196.3 0.1 select_reduce_fusion
  196.4 73.9 %all-gather.3.cloned.1.call-done = bf16[64,16,6144]{2,0,1:T(8,128)(2,1)} async-done(((bf16[64,2,6144]{2,0,1:T(8,128)(2,1)}), bf16[64,16,6144]{2,0,1:T(8,128)(2,1)}) %all-gather.3.cloned.1.call-update) | async-done | bytes 12582928 | tf_op jit(solution)/shard_map/all_gather | solution.py:52
  270.3 0.0 copy-done.2
  270.3 20.8 %fusion.14 = bf16[64,2,6144]{2,1,0:T(2,128)(2,1)} fusion(bf16[64,16,6144]{2,0,1:T(8,128)(2,1)} %all-gather.3.cloned.1.call-done, bf16[64,2,6144]{2,1,0:T(2,128)(2,1)S(1)} %copy-done.2, bf16[2,6144]{1,0:T(2,128)(2,1)S(1)} %get-tuple-element.12, pred[16]{0:T(512)(128)(4,1)S(1)} %broadcast_compare_fusion, s32[16]{0:T(128)S(1)} %select_reduce_fusion, ...), kind=kOutput, calls=%fused_computation.9 | convolution fusion | flops 28311616 | bytes 15753304 | tf_op jit(solution)/shard_map/sik,ij->sjk/dot_general | solution.py:67
  291.1 0.0 all-gather.5.cloned.1.call-update
  291.1 115.5 %all-gather.5.cloned.1.call-done = bf16[256,2,6144]{2,1,0:T(2,128)(2,1)} async-done(((bf16[64,2,6144]{2,1,0:T(2,128)(2,1)}), bf16[256,2,6144]{2,1,0:T(2,128)(2,1)}) %all-gather.5.cloned.1.call-update) | async-done | bytes 6291472 | tf_op jit(solution)/shard_map/all_gather | solution.py:72
  406.6 32.8 %fusion.12 = f32[2,256,3072]{2,1,0:T(8,128)} fusion(bf16[2,6144,3072]{2,1,0:T(8,128)(2,1)} %param.6, bf16[256,2,6144]{2,1,0:T(2,128)(2,1)} %all-gather.5.cloned.1.call-done), kind=kOutput, calls=%fused_computation.7 | convolution fusion | flops 19327352832 | bytes 88080384 | tf_op jit(solution)/shard_map/sfm,fmk->sfk/dot_general | solution.py:73
  439.4 0.0 copy-start
  439.4 3.4 fusion.20
  442.8 1.5 collective-permute-start.1
  444.3 0.0 copy-done
  444.3 2.8 copy.26
  447.0 32.3 %collective-permute-done.1 = bf16[128,2,3072]{2,0,1:T(8,128)(2,1)S(1)} collective-permute-done((bf16[128,2,3072]{2,0,1:T(8,128)(2,1)}, bf16[128,2,3072]{2,0,1:T(8,128)(2,1)S(1)}, u32[]{:S(2)}, u32[]{:S(2)}) %collective-permute-start.1) | collective-permute-done | bytes 1572896 | tf_op jit(solution)/shard_map/ppermute | solution.py:29
  479.3 2.3 fusion.18
  481.7 2.8 copy.27
  (8 shorter events, 0.1 us)
Async XLA Ops:
  7.2 188.7 %reduce-scatter.2.cloned.1.call-start = ((), (), s32[]{:S(2)}) async-start(), calls=%async_computation.1 | async-start | bytes 7864320 | tf_op jit(solution)/shard_map/reduce_scatter | solution.py:51
  7.2 37.6 %collective-permute-start = (bf16[128,2,3072]{2,1,0:T(2,128)(2,1)}, bf16[128,2,3072]{2,1,0:T(2,128)(2,1)S(1)}, u32[]{:S(2)}, u32[]{:S(2)}) collective-permute-start(bf16[128,2,3072]{2,1,0:T(2,128)(2,1)} %param.7), channel_id=1, source_target_pairs={{0,4},{4,0},{1,5},{5,1},{2,6},{6,2},{3,7},{7,3},{8,12},{12,8},{9,1... | collective-permute-start | bytes 4718600 | tf_op jit(solution)/shard_map/ppermute | solution.py:14
  83.4 112.8 %copy-start.1 = (s32[8,2]{0,1:T(2,128)S(1)}, s32[8,2]{0,1:T(2,128)}, u32[]{:S(2)}) copy-start(s32[8,2]{0,1:T(2,128)} %param.11) | copy-start | bytes 196
  83.4 112.9 %copy-start.3 = (s32[8]{0:T(128)S(1)}, s32[8]{0:T(128)}, u32[]{:S(2)}) copy-start(s32[8]{0:T(128)} %param.10) | copy-start | bytes 100
  83.4 186.9 %copy-start.2 = (bf16[64,2,6144]{2,1,0:T(2,128)(2,1)S(1)}, bf16[64,2,6144]{2,1,0:T(2,128)(2,1)}, u32[]{:S(2)}) copy-start(bf16[64,2,6144]{2,1,0:T(2,128)(2,1)} %param.8) | copy-start | bytes 4718596
  83.4 186.9 %all-gather.3.cloned.1.call-start = ((), (), s32[]{:S(2)}) async-start(), calls=%async_computation.2 | async-start | bytes 14155776 | tf_op jit(solution)/shard_map/all_gather | solution.py:52
  195.9 210.7 %all-gather.5.cloned.1.call-start = ((), (), s32[]{:S(2)}) async-start(), calls=%async_computation.3 | async-start | bytes 7864320 | tf_op jit(solution)/shard_map/all_gather | solution.py:72
  439.4 4.8 copy-start
  442.8 36.5 %collective-permute-start.1 = (bf16[128,2,3072]{2,0,1:T(8,128)(2,1)}, bf16[128,2,3072]{2,0,1:T(8,128)(2,1)S(1)}, u32[]{:S(2)}, u32[]{:S(2)}) collective-permute-start(bf16[128,2,3072]{2,0,1:T(8,128)(2,1)} %fusion.20), channel_id=1, source_target_pairs={{0,4},{4,0},{1,5},{5,1},{2,6},{6,2},{3,7},{7,3},{8,12},{12,8},{9,1... | collective-permute-start | bytes 4718600 | tf_op jit(solution)/shard_map/ppermute | solution.py:29
Sparse Core Ops, SparseCore 0:
  83.5 112.2 reduce-scatter.1
  197.7 72.4 all-gather.2
  291.2 115.3 all-gather.4
where the time goes:
time: 491 us
  waiting for transfers between devices  368 us (75%)
  matrix products  86 us (18%)
  between operations  13.8 us (3%)
  local copies, waits for them, and re-layouts  9.63 us (2%)
  other arithmetic  8.95 us (2%)
    all_gather x1, waiting for transfers between devices, shards(): gathered = lax.all_gather(combined, 'col', axis=0, tiled=True)  115 us
    reduce_scatter x1, waiting for transfers between devices, shards(): lax.psum_scatter(partial_value, 'col', scatter_dimension=0, tiled=True)  112 us
    all_gather x1, waiting for transfers between devices, shards(): portion = lax.all_gather(sampled, ('group', 'row'), axis=1, tiled=True)  73.9 us
    ppermute x1, waiting for transfers between devices, gather_row(): other = lax.ppermute(value, 'row', swap_pairs(count))  33.7 us
    dot_general x1, matrix products, shards(): jnp.einsum('sfm,fmk->sfk', gathered, fronts, preferred_element_type=jnp.f...  32.8 us
    dot_general x1, matrix products, shards(): jnp.einsum('sfk,fmk->sfm', masked, fronts, preferred_element_type=jnp.flo...  32.3 us
    ppermute x1, waiting for transfers between devices, scatter_row(): lax.ppermute(sent, 'row', swap_pairs(count)).astype(jnp.float32)  32.3 us
    dot_general x1, matrix products, shards(): jnp.einsum('sik,ij->sjk', portion, weight.astype(jnp.bfloat16), preferred...  20.8 us
  transfers between devices with their start and end apart: 5, of which 5 were waited for; matrix products, arithmetic and copies ran while one was open for 1% of the time, Pallas kernels for 0%

commit v1 on v0

--- a/solution.py
+++ b/solution.py
@@ -1,7 +1,20 @@
+import functools
+
 import jax
 import jax.numpy as jnp
 from jax import lax
+from jax.experimental import pallas as pl
+from jax.experimental.pallas import tpu as pltpu
 from jax.sharding import PartitionSpec as P
+
+PASSES = 2
+TILE = 256
+SLOTS = 6
+GATHER_SLOTS = 8
+PARTIAL_SLOTS = 4
+DRAIN = 2
+SECOND_LAG = 9
+FRONT_SLOTS = SECOND_LAG + 2
 
 
 def swap_pairs(count):
@@ -76,6 +89,539 @@
     return (sampled, projected)
 
 
+def remote(source, target, send_sem, recv_sem, device):
+    return pltpu.make_async_remote_copy(
+        src_ref=source,
+        dst_ref=target,
+        send_sem=send_sem,
+        recv_sem=recv_sem,
+        device_id=device,
+        device_id_type=pl.DeviceIdType.MESH,
+    )
+
+
+def fused(
+    cols,
+    groups,
+    samples,
+    fronts,
+    second,
+    keep,
+    from_blocks,
+    to_parents,
+    sampled,
+    projected,
+    held,
+    front_ring,
+    partial,
+    up_out,
+    up_in,
+    down_out,
+    down_in,
+    across,
+    routed,
+    gathered,
+    total,
+    product_out,
+    product_in,
+    front_sem,
+    local_sem,
+    samples_send,
+    samples_recv,
+    product_send,
+    product_recv,
+    up_send,
+    up_recv,
+    down_send,
+    down_recv,
+    across_send,
+    across_recv,
+    routed_send,
+    routed_recv,
+    above_send,
+    above_recv,
+    below_send,
+    below_recv,
+):
+    col = lax.axis_index("col")
+    row = lax.axis_index("row")
+    group = lax.axis_index("group")
+    passes, local, half, depth = samples.shape
+    block, tile = partial.shape[3:]
+    height = fronts.shape[1]
+    tiles = height // tile
+    steps = passes * tiles
+    last = cols - 1
+    other_row = 1 - row
+
+    barrier = pltpu.get_barrier_semaphore()
+
+    def greet(device):
+        pl.semaphore_signal(
+            barrier, inc=1, device_id=device, device_id_type=pl.DeviceIdType.MESH
+        )
+
+    greet({"row": other_row})
+    for shift in range(1, groups):
+        greet({"group": lax.rem(group + shift, groups)})
+
+    @pl.when(col > 0)
+    def _():
+        greet({"col": col - 1})
+
+    @pl.when(col < last)
+    def _():
+        greet({"col": col + 1})
+
+    def fetch(step):
+        slot = lax.rem(step, FRONT_SLOTS)
+        start = pl.multiple_of(lax.rem(step, tiles) * tile, tile)
+        return pltpu.make_async_copy(
+            fronts.at[:, pl.ds(start, tile), :], front_ring.at[slot], front_sem.at[slot]
+        )
+
+    for step in range(min(FRONT_SLOTS, steps)):
+        fetch(step).start()
+
+    pl.semaphore_wait(barrier, groups + jnp.minimum(col, 1) + jnp.minimum(last - col, 1))
+
+    def own_half(turn):
+        return held.at[turn, :, pl.ds(pl.multiple_of(row * half, half), half), :]
+
+    def samples_copy(turn):
+        return remote(
+            samples.at[turn],
+            own_half(turn),
+            samples_send.at[turn],
+            samples_recv.at[turn],
+            {"row": other_row},
+        )
+
+    def samples_here(turn):
+        return pltpu.make_async_copy(samples.at[turn], own_half(turn), local_sem.at[turn])
+
+    for turn in range(passes):
+        samples_copy(turn).start()
+        samples_here(turn).start()
+
+    total[...] = jnp.zeros_like(total)
+
+    def live(step):
+        return (step >= 0) & (step < steps)
+
+    def spent(step):
+        return (step >= DRAIN) & (step < steps + DRAIN)
+
+    def up_copy(step, chunk):
+        slot = lax.rem(step, SLOTS)
+        return remote(
+            up_out.at[slot, chunk],
+            up_in.at[slot, chunk],
+            up_send.at[slot, chunk],
+            up_recv.at[slot, chunk],
+            {"col": jnp.minimum(col + 1, last)},
+        )
+
+    def down_copy(step, chunk):
+        slot = lax.rem(step, SLOTS)
+        return remote(
+            down_out.at[slot, chunk],
+            down_in.at[slot, chunk],
+            down_send.at[slot, chunk],
+            down_recv.at[slot, chunk],
+            {"col": jnp.maximum(col - 1, 0)},
+        )
+
+    def across_copy(step):
+        slot = lax.rem(step, SLOTS)
+        return remote(
+            across.at[slot, row],
+            across.at[slot, row],
+            across_send.at[slot],
+            across_recv.at[slot],
+            {"row": other_row},
+        )
+
+    def routed_copy(step, shift):
+        slot = lax.rem(step, SLOTS)
+        return remote(
+            routed.at[slot, group],
+            routed.at[slot, group],
+            routed_send.at[slot, shift],
+            routed_recv.at[slot, shift],
+            {"group": lax.rem(group + shift, groups)},
+        )
+
+    def above_copy(step, chunk):
+        slot = lax.rem(step, GATHER_SLOTS)
+        return remote(
+            gathered.at[slot, :, chunk],
+            gathered.at[slot, :, chunk],
+            above_send.at[slot, chunk],
+            above_recv.at[slot, chunk],
+            {"col": jnp.minimum(col + 1, last)},
+        )
+
+    def below_copy(step, chunk):
+        slot = lax.rem(step, GATHER_SLOTS)
+        return remote(
+            gathered.at[slot, :, chunk],
+            gathered.at[slot, :, chunk],
+            below_send.at[slot, chunk],
+            below_recv.at[slot, chunk],
+            {"col": jnp.maximum(col - 1, 0)},
+        )
+
+    def first_product(step):
+        @pl.when(live(step))
+        def _():
+            turn = step // tiles
+
+            @pl.when(lax.rem(step, tiles) == 0)
+            def _():
+                samples_here(turn).wait()
+                samples_copy(turn).wait_recv()
+
+            fetch(step).wait()
+            slot = lax.rem(step, FRONT_SLOTS)
+            into = lax.rem(step, PARTIAL_SLOTS)
+            for front in range(local):
+                value = lax.dot_general(
+                    held[turn, front],
+                    front_ring[slot, front],
+                    (((1,), (1,)), ((), ())),
+                    preferred_element_type=jnp.float32,
+                )
+                for chunk in range(cols):
+                    partial[into, chunk, front] = value[chunk * block : (chunk + 1) * block]
+
+    def hop(step, toward, edge, copy, out, received):
+        @pl.when(spent(step))
+        def _():
+            for chunk in range(cols):
+
+                @pl.when(toward(chunk))
+                def _():
+                    copy(step - DRAIN, chunk).wait_send()
+
+        @pl.when(live(step))
+        def _():
+            slot = lax.rem(step, SLOTS)
+            own = lax.rem(step, PARTIAL_SLOTS)
+            for chunk in range(cols):
+
+                @pl.when(toward(chunk))
+                def _():
+                    @pl.when(col == edge)
+                    def _():
+                        out[slot, chunk] = partial[own, chunk].astype(out.dtype)
+
+                    @pl.when(col != edge)
+                    def _():
+                        copy(step, chunk).wait_recv()
+                        out[slot, chunk] = (
+                            partial[own, chunk] + received[slot, chunk].astype(jnp.float32)
+                        ).astype(out.dtype)
+
+                    copy(step, chunk).start()
+
+    def finish(step):
+        @pl.when(spent(step))
+        def _():
+            across_copy(step - DRAIN).wait_send()
+
+        @pl.when(live(step))
+        def _():
+            slot = lax.rem(step, SLOTS)
+            own = lax.rem(step, PARTIAL_SLOTS)
+            turn = step // tiles
+            lanes = pl.ds(pl.multiple_of(lax.rem(step, tiles) * tile, tile), tile)
+
+            def store(value):
+                for front in range(local):
+                    out = (value[front] * keep[front : front + 1, lanes]).astype(sampled.dtype)
+                    sampled[front, turn, :, lanes] = out
+                    across[slot, row, front] = out
+
+            @pl.when(col == 0)
+            def _():
+                down_copy(step, col).wait_recv()
+                store(partial[own, col] + down_in[slot, col].astype(jnp.float32))
+
+            @pl.when(col == last)
+            def _():
+                up_copy(step, col).wait_recv()
+                store(partial[own, col] + up_in[slot, col].astype(jnp.float32))
+
+            @pl.when((col > 0) & (col < last))
+            def _():
+                up_copy(step, col).wait_recv()
+                down_copy(step, col).wait_recv()
+                store(
+                    partial[own, col]
+                    + up_in[slot, col].astype(jnp.float32)
+                    + down_in[slot, col].astype(jnp.float32)
+                )
+
+            across_copy(step).start()
+
+    def route(step):
+        @pl.when(spent(step))
+        def _():
+            for shift in range(1, groups):
+                routed_copy(step - DRAIN, shift).wait_send()
+
+        @pl.when(live(step))
+        def _():
+            slot = lax.rem(step, SLOTS)
+            across_copy(step).wait_recv()
+            for front in range(local):
+                value = from_blocks[front, 0] * across[slot, 0, front].astype(jnp.float32)
+                value += from_blocks[front, 1] * across[slot, 1, front].astype(jnp.float32)
+                routed[slot, group, front] = value.astype(routed.dtype)
+            for shift in range(1, groups):
+                routed_copy(step, shift).start()
+
+    def send_chunk(step, chunk):
+        @pl.when(col < last)
+        def _():
+            above_copy(step, chunk).start()
+
+        @pl.when(col > 0)
+        def _():
+            below_copy(step, chunk).start()
+
+    def drain_chunk(step, chunk):
+        @pl.when(col < last)
+        def _():
+            above_copy(step, chunk).wait_send()
+
+        @pl.when(col > 0)
+        def _():
+            below_copy(step, chunk).wait_send()
+
+    def combine(step):
+        @pl.when(spent(step))
+        def _():
+            drain_chunk(step - DRAIN, col)
+
+        @pl.when(live(step))
+        def _():
+            slot = lax.rem(step, SLOTS)
+            turn = step // tiles
+            lanes = pl.ds(pl.multiple_of(lax.rem(step, tiles) * tile, tile), tile)
+            for shift in range(1, groups):
+                routed_copy(step, shift).wait_recv()
+            parts = [
+                routed[slot, source, front].astype(jnp.float32)
+                for source in range(groups)
+                for front in range(local)
+            ]
+            for parent in range(local):
+                value = second[parent, turn, :, lanes].astype(jnp.float32)
+                for number, part in enumerate(parts):
+                    value += to_parents[parent, number] * part
+                value = value * keep[parent : parent + 1, lanes]
+                gathered[lax.rem(step, GATHER_SLOTS), parent, col] = value.astype(gathered.dtype)
+            send_chunk(step, col)
+
+    def forward(step, far):
+        @pl.when((col >= far) & (col < last))
+        def _():
+            @pl.when(spent(step))
+            def _():
+                above_copy(step - DRAIN, col - far).wait_send()
+
+        @pl.when((col + far <= last) & (col > 0))
+        def _():
+            @pl.when(spent(step))
+            def _():
+                below_copy(step - DRAIN, col + far).wait_send()
+
+        @pl.when(live(step))
+        def _():
+            @pl.when(col >= far)
+            def _():
+                above_copy(step, col - far).wait_recv()
+
+                @pl.when(col < last)
+                def _():
+                    above_copy(step, col - far).start()
+
+            @pl.when(col + far <= last)
+            def _():
+                below_copy(step, col + far).wait_recv()
+
+                @pl.when(col > 0)
+                def _():
+                    below_copy(step, col + far).start()
+
+    def product_copy(turn):
+        return remote(
+            product_out.at[turn],
+            product_in.at[turn],
+            product_send.at[turn],
+            product_recv.at[turn],
+            {"row": other_row},
+        )
+
+    def second_product(step):
+        @pl.when(live(step))
+        def _():
+            @pl.when(col == last)
+            def _():
+                above_copy(step, col - last).wait_recv()
+
+            @pl.when(col == 0)
+            def _():
+                below_copy(step, col + last).wait_recv()
+
+            turn = step // tiles
+            slot = lax.rem(step, FRONT_SLOTS)
+            from_slot = lax.rem(step, GATHER_SLOTS)
+            width = depth // 6 if depth % 768 == 0 else depth
+            for front in range(local):
+                rows = gathered[from_slot, front].reshape(cols * block, tile)
+                for begin in range(0, depth, width):
+                    total[turn, front, :, begin : begin + width] += jnp.dot(
+                        rows,
+                        front_ring[slot, front, :, begin : begin + width],
+                        preferred_element_type=jnp.float32,
+                    )
+
+            @pl.when(lax.rem(step, tiles) == tiles - 1)
+            def _():
+                theirs = pl.ds(pl.multiple_of(other_row * half, half), half)
+                for front in range(local):
+                    product_out[turn, front] = total[turn, front, theirs].astype(
+                        product_out.dtype
+                    )
+                product_copy(turn).start()
+
+            @pl.when(step + FRONT_SLOTS < steps)
+            def _():
+                fetch(step + FRONT_SLOTS).start()
+
+    @pl.loop(0, steps + SECOND_LAG)
+    def _(time):
+        first_product(time)
+        hop(time - col, lambda chunk: chunk > col, 0, up_copy, up_out, up_in)
+        hop(time - (last - col), lambda chunk: chunk < col, last, down_copy, down_out, down_in)
+        finish(time - last)
+        second_product(time - SECOND_LAG)
+        route(time - last - 1)
+        combine(time - last - 2)
+        for far in range(1, last):
+            forward(time - last - 2 - far, far)
+
+    for turn in range(passes):
+        product_copy(turn).wait_recv()
+        ours = pl.ds(pl.multiple_of(row * half, half), half)
+        for front in range(local):
+            projected[turn, front] = (
+                total[turn, front, ours] + product_in[turn, front].astype(jnp.float32)
+            ).astype(projected.dtype)
+        product_copy(turn).wait_send()
+        samples_copy(turn).wait_send()
+
+
+def pipeline(fronts, samples, second_samples, front_sizes, parent_ids, block_maps):
+    local, height, depth = fronts.shape
+    groups, cols = lax.axis_size("group"), lax.axis_size("col")
+    group, row, col = lax.axis_index("group"), lax.axis_index("row"), lax.axis_index("col")
+    number, block_count = block_maps.shape
+    own_sizes = lax.dynamic_slice_in_dim(front_sizes, group * local, local, 0)
+    row_keep = row * height + jnp.arange(height, dtype=jnp.int32)[None, :] < own_sizes[:, None]
+    col_keep = col * depth + jnp.arange(depth, dtype=jnp.int32)[None, :] < own_sizes[:, None]
+    own_fronts = group * local + jnp.arange(local, dtype=jnp.int32)
+
+    block = second_samples.shape[0] // PASSES
+    half = samples.shape[0] // PASSES
+    first = samples * col_keep[None].astype(samples.dtype)
+    first = first.reshape(half // block, PASSES, block, local, depth)
+    first = first.transpose(1, 3, 0, 2, 4).reshape(PASSES, local, half, depth)
+    second = second_samples.reshape(PASSES, block, local, height).transpose(2, 0, 1, 3)
+    own_maps = lax.dynamic_slice_in_dim(block_maps, group * local, local, 0)
+    from_blocks = (own_maps == row).astype(jnp.float32)
+    to_parents = (own_fronts[:, None] == parent_ids[None, :]).astype(jnp.float32)
+
+    def vmem(*shape, dtype=jnp.bfloat16):
+        return pltpu.VMEM(shape, dtype)
+
+    def sems(*shape):
+        return pltpu.SemaphoreType.DMA(shape)
+
+    in_vmem = pl.BlockSpec(memory_space=pltpu.VMEM)
+    in_smem = pl.BlockSpec(memory_space=pltpu.SMEM)
+    anywhere = pl.BlockSpec(memory_space=pl.ANY)
+    f32 = jnp.float32
+    sampled, projected = pl.pallas_call(
+        functools.partial(fused, cols, groups),
+        out_shape=(
+            jax.ShapeDtypeStruct((local, PASSES, block, height), jnp.bfloat16),
+            jax.ShapeDtypeStruct((PASSES, local, half, depth), jnp.bfloat16),
+        ),
+        in_specs=[anywhere, anywhere, in_vmem, in_vmem, in_smem, in_smem],
+        out_specs=(in_vmem, in_vmem),
+        scratch_shapes=[
+            vmem(PASSES, local, 2 * half, depth),
+            vmem(FRONT_SLOTS, local, TILE, depth),
+            vmem(PARTIAL_SLOTS, cols, local, block, TILE, dtype=f32),
+            vmem(SLOTS, cols, local, block, TILE),
+            vmem(SLOTS, cols, local, block, TILE),
+            vmem(SLOTS, cols, local, block, TILE),
+            vmem(SLOTS, cols, local, block, TILE),
+            vmem(SLOTS, 2, local, block, TILE),
+            vmem(SLOTS, groups, local, block, TILE),
+            vmem(GATHER_SLOTS, local, cols, block, TILE),
+            vmem(PASSES, local, 2 * half, depth, dtype=f32),
+            vmem(PASSES, local, half, depth),
+            vmem(PASSES, local, half, depth),
+            sems(FRONT_SLOTS),
+            sems(PASSES),
+            sems(PASSES),
+            sems(PASSES),
+            sems(PASSES),
+            sems(PASSES),
+            sems(SLOTS, cols),
+            sems(SLOTS, cols),
+            sems(SLOTS, cols),
+            sems(SLOTS, cols),
+            sems(SLOTS),
+            sems(SLOTS),
+            sems(SLOTS, groups),
+            sems(SLOTS, groups),
+            sems(GATHER_SLOTS, cols),
+            sems(GATHER_SLOTS, cols),
+            sems(GATHER_SLOTS, cols),
+            sems(GATHER_SLOTS, cols),
+        ],
+        compiler_params=pltpu.CompilerParams(
+            collective_id=0, has_side_effects=True, vmem_limit_bytes=67043328
+        ),
+    )(first, fronts, second, row_keep.astype(f32), from_blocks, to_parents)
+    sampled = sampled.transpose(1, 2, 0, 3).reshape(second_samples.shape)
+    projected = projected.reshape(PASSES, local, half // block, block, depth)
+    projected = projected.transpose(2, 0, 3, 1, 4).reshape(samples.shape)
+    projected = projected * col_keep[None].astype(projected.dtype)
+    return sampled, projected
+
+
+def fits(mesh, fronts, samples, second_samples, block_maps):
+    rows, cols = mesh.shape["row"], mesh.shape["col"]
+    height, depth = fronts.shape[1] // rows, fronts.shape[2] // cols
+    block = second_samples.shape[0] // cols // PASSES
+    return (
+        rows == 2
+        and cols == 4
+        and block_maps.shape[1] == rows
+        and height % TILE == 0
+        and depth % 128 == 0
+        and second_samples.shape[0] % (cols * PASSES) == 0
+        and block % 16 == 0
+    )
+
+
 def solution(mesh):
     placed = (
         P("group", "row", "col"),
@@ -85,10 +631,15 @@
         P(),
         P(),
     )
-    return jax.shard_map(
-        shards,
-        mesh=mesh,
-        in_specs=placed,
-        out_specs=(P("col", "group", "row"), P("row", "group", "col")),
-        check_vma=False,
-    )
+
+    def step(fronts, samples, second_samples, front_sizes, parent_ids, block_maps):
+        fast = fits(mesh, fronts, samples, second_samples, block_maps)
+        return jax.shard_map(
+            pipeline if fast else shards,
+            mesh=mesh,
+            in_specs=placed,
+            out_specs=(P("col", "group", "row"), P("row", "group", "col")),
+            check_vma=False,
+        )(fronts, samples, second_samples, front_sizes, parent_ids, block_maps)
+
+    return step

time: 491 us -> 263 us (0.54)
  waiting for transfers between devices: 368 us -> 0 us
  Pallas kernels: 0 us -> 244 us
  matrix products: 86 us -> 0 us
  between operations: 13.8 us -> 0.72 us
    pallas_call x0 -> x1, Pallas kernels: none -> 244 us  [pipeline(): pl.pallas_call(functools.partial(fused, cols, groups), out_shape=(jax.Sha...]
    all_gather x2 -> x0, waiting for transfers between devices: 189 us -> none  [the longest x1 115 us: shards(): gathered = lax.all_gather(combined, 'col', axis=0, tiled=True)]
    reduce_scatter x1 -> x0, waiting for transfers between devices: 112 us -> none  [shards(): lax.psum_scatter(partial_value, 'col', scatter_dimension=0, tiled=True)]
    dot_general x3 -> x0, matrix products: 86 us -> none  [the longest x1 32.8 us: shards(): jnp.einsum('sfm,fmk->sfk', gathered, fronts, preferred_element_type=jnp.f...]
    ppermute x2 -> x0, waiting for transfers between devices: 65.9 us -> none  [the longest x1 33.7 us: gather_row(): other = lax.ppermute(value, 'row', swap_pairs(count))]
  transfers between devices with their start and end apart: 5 -> 0, of which waited for: 5 -> 0; matrix products, arithmetic and copies ran while one was open for 1% -> 0% of each run, Pallas kernels for 0% -> 0%
where the time goes in v1:
time: 263 us
  Pallas kernels  244 us (93%)
  local copies, waits for them, and re-layouts  10.8 us (4%)
  other arithmetic  6.68 us (3%)
    pallas_call x1, Pallas kernels, pipeline(): pl.pallas_call(functools.partial(fused, cols, groups), out_shape=(jax.Sha...  244 us
    unnamed x12, local copies, waits for them, and re-layouts  6.18 us

profile of v1, /device:TPU:0, one launch (start us, length us, event | category | flops | bytes accessed | tf_op | source)
XLA Modules:
  0.0 262.5 jit_solution(16084864979764439457)
XLA Ops:
  0.6 0.7 dynamic_slice.6
  1.4 0.7 constant_dynamic-slice_fusion
  2.1 0.1 copy.13
  2.2 0.5 compare_convert_fusion.3.from_blocks
  2.8 1.3 compare_convert_fusion.2.to_parents
  4.1 0.1 compare_convert_fusion.1
  4.1 0.0 copy-start.2
  4.2 0.7 compare_convert_fusion.keep
  4.9 0.0 copy-done.2
  4.9 1.5 broadcast_multiply_fusion
  6.4 0.0 copy-start
  6.5 1.5 copy.8
  8.0 0.1 copy-done
  8.1 1.6 copy.9
  9.7 244.3 %shard_map.77 = (bf16[2,2,32,6144]{3,2,1,0:T(8,128)(2,1)}, bf16[2,2,64,3072]{3,2,1,0:T(8,128)(2,1)}) custom-call(bf16[2,2,64,3072]{3,2,1,0:T(8,128)(2,1)} %bitcast.19, bf16[2,6144,3072]{2,1,0:T(8,128)(2,1)} %fronts.1, bf16[2,2,32,6144]{3,2,1,0:T(8,128)(2,1)} %bitcast.20, f32[2,6144]{1,0:T(2,128)} %compare_convert_fusion.keep, ...), custom_call_target="tpu_custom_call" | custom-call | tf_op jit(solution)/shard_map/pallas_call | solution.py:558
  254.1 0.0 copy-start.1
  254.1 4.3 %copy.12 = bf16[64,2,6144]{2,1,0:T(2,128)(2,1)} copy(bf16[64,2,6144]{2,0,1:T(8,128)(2,1)} %bitcast.23) | data formatting | bytes 3145728
  258.4 0.0 copy-done.1
  258.4 0.0 copy-start.3
  258.4 1.6 copy.11
  260.0 0.0 copy-done.3
  260.0 2.5 bitcast_multiply_fusion
  (4 shorter events, 0.0 us)
Async XLA Ops:
  4.1 0.8 copy-start.2
  6.4 1.6 copy-start
  254.1 4.3 %copy-start.1 = (bf16[2,2,64,3072]{3,2,1,0:T(8,128)(2,1)S(1)}, bf16[2,2,64,3072]{3,2,1,0:T(8,128)(2,1)}, u32[]{:S(2)}) copy-start(bf16[2,2,64,3072]{3,2,1,0:T(8,128)(2,1)} %get-tuple-element.5) | copy-start | bytes 4718596
  258.4 1.6 copy-start.3

commit v2 on v1

--- a/solution.py
+++ b/solution.py
@@ -9,12 +9,18 @@
 
 PASSES = 2
 TILE = 256
-SLOTS = 6
-GATHER_SLOTS = 8
-PARTIAL_SLOTS = 4
+BLOCK_TILES = 6
+HOP = 2
+ROUTE_LAG = 3 * HOP + 1
+COMBINE_LAG = ROUTE_LAG + 2
+SECOND_LAG = COMBINE_LAG + 3 * HOP
+SLOTS = 8
+OUT_SLOTS = 4
+IN_SLOTS = 10
+GATHER_SLOTS = 12
+PARTIAL_SLOTS = 3 * HOP + 1
 DRAIN = 2
-SECOND_LAG = 9
-FRONT_SLOTS = SECOND_LAG + 2
+FRONT_SLOTS = 12
 
 
 def swap_pairs(count):
@@ -105,10 +111,13 @@
     groups,
     samples,
     fronts,
+    second_from,
+    sizes,
+    parents,
+    maps,
+    sampled_to,
+    projected_to,
     second,
-    keep,
-    from_blocks,
-    to_parents,
     sampled,
     projected,
     held,
@@ -126,6 +135,9 @@
     product_in,
     front_sem,
     local_sem,
+    second_sem,
+    sampled_sem,
+    projected_sem,
     samples_send,
     samples_recv,
     product_send,
@@ -152,6 +164,7 @@
     tiles = height // tile
     steps = passes * tiles
     last = cols - 1
+    run = BLOCK_TILES
     other_row = 1 - row
 
     barrier = pltpu.get_barrier_semaphore()
@@ -173,15 +186,34 @@
     def _():
         greet({"col": col + 1})
 
-    def fetch(step):
-        slot = lax.rem(step, FRONT_SLOTS)
-        start = pl.multiple_of(lax.rem(step, tiles) * tile, tile)
+    def place(step):
+        begin = lax.div(step, passes * run)
+        rest = lax.rem(step, passes * run)
+        return lax.div(rest, run), begin * run + lax.rem(rest, run)
+
+    def lanes_of(spot):
+        return pl.ds(pl.multiple_of(spot * tile, tile), tile)
+
+    def fetch(spot):
+        slot = lax.rem(spot, FRONT_SLOTS)
+        start = pl.multiple_of(spot * tile, tile)
         return pltpu.make_async_copy(
             fronts.at[:, pl.ds(start, tile), :], front_ring.at[slot], front_sem.at[slot]
         )
 
-    for step in range(min(FRONT_SLOTS, steps)):
-        fetch(step).start()
+    own_fronts = [group * local + front for front in range(local)]
+    own_sizes = [sizes[front] for front in own_fronts]
+    number = parents.shape[0]
+
+    def weight(condition):
+        return jnp.where(condition, 1.0, 0.0).astype(jnp.float32)
+
+    def kept(front, start, shape):
+        at = start + lax.broadcasted_iota(jnp.int32, shape, len(shape) - 1)
+        return at < own_sizes[front]
+
+    second_copy = pltpu.make_async_copy(second_from, second, second_sem)
+    sampled_copy = pltpu.make_async_copy(sampled, sampled_to, sampled_sem)
 
     pl.semaphore_wait(barrier, groups + jnp.minimum(col, 1) + jnp.minimum(last - col, 1))
 
@@ -203,7 +235,9 @@
     for turn in range(passes):
         samples_copy(turn).start()
         samples_here(turn).start()
-
+    for spot in range(min(FRONT_SLOTS, tiles)):
+        fetch(spot).start()
+    second_copy.start()
     total[...] = jnp.zeros_like(total)
 
     def live(step):
@@ -213,22 +247,22 @@
         return (step >= DRAIN) & (step < steps + DRAIN)
 
     def up_copy(step, chunk):
-        slot = lax.rem(step, SLOTS)
+        slot, into = lax.rem(step, OUT_SLOTS), lax.rem(step, IN_SLOTS)
         return remote(
             up_out.at[slot, chunk],
-            up_in.at[slot, chunk],
+            up_in.at[into, chunk],
             up_send.at[slot, chunk],
-            up_recv.at[slot, chunk],
+            up_recv.at[into, chunk],
             {"col": jnp.minimum(col + 1, last)},
         )
 
     def down_copy(step, chunk):
-        slot = lax.rem(step, SLOTS)
+        slot, into = lax.rem(step, OUT_SLOTS), lax.rem(step, IN_SLOTS)
         return remote(
             down_out.at[slot, chunk],
-            down_in.at[slot, chunk],
+            down_in.at[into, chunk],
             down_send.at[slot, chunk],
-            down_recv.at[slot, chunk],
+            down_recv.at[into, chunk],
             {"col": jnp.maximum(col - 1, 0)},
         )
 
@@ -275,15 +309,22 @@
     def first_product(step):
         @pl.when(live(step))
         def _():
-            turn = step // tiles
-
-            @pl.when(lax.rem(step, tiles) == 0)
+            turn, spot = place(step)
+
+            @pl.when(spot == 0)
             def _():
                 samples_here(turn).wait()
                 samples_copy(turn).wait_recv()
-
-            fetch(step).wait()
-            slot = lax.rem(step, FRONT_SLOTS)
+                for front in range(local):
+                    value = held[turn, front]
+                    kept_here = kept(front, col * depth, value.shape)
+                    held[turn, front] = jnp.where(kept_here, value, jnp.zeros_like(value))
+
+            @pl.when(turn == 0)
+            def _():
+                fetch(spot).wait()
+
+            slot = lax.rem(spot, FRONT_SLOTS)
             into = lax.rem(step, PARTIAL_SLOTS)
             for front in range(local):
                 value = lax.dot_general(
@@ -295,7 +336,7 @@
                 for chunk in range(cols):
                     partial[into, chunk, front] = value[chunk * block : (chunk + 1) * block]
 
-    def hop(step, toward, edge, copy, out, received):
+    def hop(step, order, toward, edge, copy, out, received):
         @pl.when(spent(step))
         def _():
             for chunk in range(cols):
@@ -306,9 +347,9 @@
 
         @pl.when(live(step))
         def _():
-            slot = lax.rem(step, SLOTS)
+            slot, into = lax.rem(step, OUT_SLOTS), lax.rem(step, IN_SLOTS)
             own = lax.rem(step, PARTIAL_SLOTS)
-            for chunk in range(cols):
+            for chunk in order:
 
                 @pl.when(toward(chunk))
                 def _():
@@ -320,7 +361,7 @@
                     def _():
                         copy(step, chunk).wait_recv()
                         out[slot, chunk] = (
-                            partial[own, chunk] + received[slot, chunk].astype(jnp.float32)
+                            partial[own, chunk] + received[into, chunk].astype(jnp.float32)
                         ).astype(out.dtype)
 
                     copy(step, chunk).start()
@@ -332,26 +373,27 @@
 
         @pl.when(live(step))
         def _():
-            slot = lax.rem(step, SLOTS)
+            slot, into = lax.rem(step, SLOTS), lax.rem(step, IN_SLOTS)
             own = lax.rem(step, PARTIAL_SLOTS)
-            turn = step // tiles
-            lanes = pl.ds(pl.multiple_of(lax.rem(step, tiles) * tile, tile), tile)
+            turn, spot = place(step)
+            lanes = lanes_of(spot)
 
             def store(value):
                 for front in range(local):
-                    out = (value[front] * keep[front : front + 1, lanes]).astype(sampled.dtype)
+                    kept_here = kept(front, row * height + spot * tile, (block, tile))
+                    out = jnp.where(kept_here, value[front], 0.0).astype(sampled.dtype)
                     sampled[front, turn, :, lanes] = out
                     across[slot, row, front] = out
 
             @pl.when(col == 0)
             def _():
                 down_copy(step, col).wait_recv()
-                store(partial[own, col] + down_in[slot, col].astype(jnp.float32))
+                store(partial[own, col] + down_in[into, col].astype(jnp.float32))
 
             @pl.when(col == last)
             def _():
                 up_copy(step, col).wait_recv()
-                store(partial[own, col] + up_in[slot, col].astype(jnp.float32))
+                store(partial[own, col] + up_in[into, col].astype(jnp.float32))
 
             @pl.when((col > 0) & (col < last))
             def _():
@@ -359,11 +401,15 @@
                 down_copy(step, col).wait_recv()
                 store(
                     partial[own, col]
-                    + up_in[slot, col].astype(jnp.float32)
-                    + down_in[slot, col].astype(jnp.float32)
+                    + up_in[into, col].astype(jnp.float32)
+                    + down_in[into, col].astype(jnp.float32)
                 )
 
             across_copy(step).start()
+
+            @pl.when(step == steps - 1)
+            def _():
+                sampled_copy.start()
 
     def route(step):
         @pl.when(spent(step))
@@ -376,8 +422,9 @@
             slot = lax.rem(step, SLOTS)
             across_copy(step).wait_recv()
             for front in range(local):
-                value = from_blocks[front, 0] * across[slot, 0, front].astype(jnp.float32)
-                value += from_blocks[front, 1] * across[slot, 1, front].astype(jnp.float32)
+                at = own_fronts[front]
+                value = weight(maps[0, at] == row) * across[slot, 0, front].astype(jnp.float32)
+                value += weight(maps[1, at] == row) * across[slot, 1, front].astype(jnp.float32)
                 routed[slot, group, front] = value.astype(routed.dtype)
             for shift in range(1, groups):
                 routed_copy(step, shift).start()
@@ -408,8 +455,12 @@
         @pl.when(live(step))
         def _():
             slot = lax.rem(step, SLOTS)
-            turn = step // tiles
-            lanes = pl.ds(pl.multiple_of(lax.rem(step, tiles) * tile, tile), tile)
+            turn, spot = place(step)
+            lanes = lanes_of(spot)
+            @pl.when(step == 0)
+            def _():
+                second_copy.wait()
+
             for shift in range(1, groups):
                 routed_copy(step, shift).wait_recv()
             parts = [
@@ -419,9 +470,11 @@
             ]
             for parent in range(local):
                 value = second[parent, turn, :, lanes].astype(jnp.float32)
-                for number, part in enumerate(parts):
-                    value += to_parents[parent, number] * part
-                value = value * keep[parent : parent + 1, lanes]
+                for child in range(number):
+                    value += weight(parents[child] == own_fronts[parent]) * parts[child]
+                value = jnp.where(
+                    kept(parent, row * height + spot * tile, value.shape), value, 0.0
+                )
                 gathered[lax.rem(step, GATHER_SLOTS), parent, col] = value.astype(gathered.dtype)
             send_chunk(step, col)
 
@@ -440,21 +493,15 @@
 
         @pl.when(live(step))
         def _():
-            @pl.when(col >= far)
+            @pl.when((col >= far) & (col < last))
             def _():
                 above_copy(step, col - far).wait_recv()
-
-                @pl.when(col < last)
-                def _():
-                    above_copy(step, col - far).start()
-
-            @pl.when(col + far <= last)
+                above_copy(step, col - far).start()
+
+            @pl.when((col + far <= last) & (col > 0))
             def _():
                 below_copy(step, col + far).wait_recv()
-
-                @pl.when(col > 0)
-                def _():
-                    below_copy(step, col + far).start()
+                below_copy(step, col + far).start()
 
     def product_copy(turn):
         return remote(
@@ -470,14 +517,16 @@
         def _():
             @pl.when(col == last)
             def _():
-                above_copy(step, col - last).wait_recv()
+                for chunk in range(last):
+                    above_copy(step, chunk).wait_recv()
 
             @pl.when(col == 0)
             def _():
-                below_copy(step, col + last).wait_recv()
-
-            turn = step // tiles
-            slot = lax.rem(step, FRONT_SLOTS)
+                for chunk in range(1, cols):
+                    below_copy(step, chunk).wait_recv()
+
+            turn, spot = place(step)
+            slot = lax.rem(spot, FRONT_SLOTS)
             from_slot = lax.rem(step, GATHER_SLOTS)
             width = depth // 6 if depth % 768 == 0 else depth
             for front in range(local):
@@ -489,7 +538,7 @@
                         preferred_element_type=jnp.float32,
                     )
 
-            @pl.when(lax.rem(step, tiles) == tiles - 1)
+            @pl.when(spot == tiles - 1)
             def _():
                 theirs = pl.ds(pl.multiple_of(other_row * half, half), half)
                 for front in range(local):
@@ -498,60 +547,56 @@
                     )
                 product_copy(turn).start()
 
-            @pl.when(step + FRONT_SLOTS < steps)
-            def _():
-                fetch(step + FRONT_SLOTS).start()
+            @pl.when((turn == passes - 1) & (spot + FRONT_SLOTS < tiles))
+            def _():
+                fetch(spot + FRONT_SLOTS).start()
 
     @pl.loop(0, steps + SECOND_LAG)
     def _(time):
         first_product(time)
-        hop(time - col, lambda chunk: chunk > col, 0, up_copy, up_out, up_in)
-        hop(time - (last - col), lambda chunk: chunk < col, last, down_copy, down_out, down_in)
-        finish(time - last)
+        hop(time - HOP * col, range(cols - 1, -1, -1), lambda chunk: chunk > col, 0, up_copy, up_out, up_in)
+        hop(time - HOP * (last - col), range(cols), lambda chunk: chunk < col, last, down_copy, down_out, down_in)
+        finish(time - HOP * last)
         second_product(time - SECOND_LAG)
-        route(time - last - 1)
-        combine(time - last - 2)
+        route(time - ROUTE_LAG)
+        combine(time - COMBINE_LAG)
         for far in range(1, last):
-            forward(time - last - 2 - far, far)
+            forward(time - COMBINE_LAG - HOP * far, far)
+
+    def projected_copy(turn):
+        return pltpu.make_async_copy(
+            projected.at[turn], projected_to.at[turn], projected_sem.at[turn]
+        )
 
     for turn in range(passes):
         product_copy(turn).wait_recv()
         ours = pl.ds(pl.multiple_of(row * half, half), half)
         for front in range(local):
-            projected[turn, front] = (
-                total[turn, front, ours] + product_in[turn, front].astype(jnp.float32)
-            ).astype(projected.dtype)
+            value = total[turn, front, ours] + product_in[turn, front].astype(jnp.float32)
+            kept_here = kept(front, col * depth, value.shape)
+            projected[turn, front] = jnp.where(kept_here, value, 0.0).astype(projected.dtype)
+        projected_copy(turn).start()
+    for turn in range(passes):
         product_copy(turn).wait_send()
         samples_copy(turn).wait_send()
+        projected_copy(turn).wait()
+    sampled_copy.wait()
 
 
 def pipeline(fronts, samples, second_samples, front_sizes, parent_ids, block_maps):
     local, height, depth = fronts.shape
     groups, cols = lax.axis_size("group"), lax.axis_size("col")
-    group, row, col = lax.axis_index("group"), lax.axis_index("row"), lax.axis_index("col")
-    number, block_count = block_maps.shape
-    own_sizes = lax.dynamic_slice_in_dim(front_sizes, group * local, local, 0)
-    row_keep = row * height + jnp.arange(height, dtype=jnp.int32)[None, :] < own_sizes[:, None]
-    col_keep = col * depth + jnp.arange(depth, dtype=jnp.int32)[None, :] < own_sizes[:, None]
-    own_fronts = group * local + jnp.arange(local, dtype=jnp.int32)
-
     block = second_samples.shape[0] // PASSES
     half = samples.shape[0] // PASSES
-    first = samples * col_keep[None].astype(samples.dtype)
-    first = first.reshape(half // block, PASSES, block, local, depth)
+    first = samples.reshape(half // block, PASSES, block, local, depth)
     first = first.transpose(1, 3, 0, 2, 4).reshape(PASSES, local, half, depth)
     second = second_samples.reshape(PASSES, block, local, height).transpose(2, 0, 1, 3)
-    own_maps = lax.dynamic_slice_in_dim(block_maps, group * local, local, 0)
-    from_blocks = (own_maps == row).astype(jnp.float32)
-    to_parents = (own_fronts[:, None] == parent_ids[None, :]).astype(jnp.float32)
-
     def vmem(*shape, dtype=jnp.bfloat16):
         return pltpu.VMEM(shape, dtype)
 
     def sems(*shape):
         return pltpu.SemaphoreType.DMA(shape)
 
-    in_vmem = pl.BlockSpec(memory_space=pltpu.VMEM)
     in_smem = pl.BlockSpec(memory_space=pltpu.SMEM)
     anywhere = pl.BlockSpec(memory_space=pl.ANY)
     f32 = jnp.float32
@@ -561,16 +606,19 @@
             jax.ShapeDtypeStruct((local, PASSES, block, height), jnp.bfloat16),
             jax.ShapeDtypeStruct((PASSES, local, half, depth), jnp.bfloat16),
         ),
-        in_specs=[anywhere, anywhere, in_vmem, in_vmem, in_smem, in_smem],
-        out_specs=(in_vmem, in_vmem),
+        in_specs=[anywhere, anywhere, anywhere, in_smem, in_smem, in_smem],
+        out_specs=(anywhere, anywhere),
         scratch_shapes=[
+            vmem(local, PASSES, block, height),
+            vmem(local, PASSES, block, height),
+            vmem(PASSES, local, half, depth),
             vmem(PASSES, local, 2 * half, depth),
             vmem(FRONT_SLOTS, local, TILE, depth),
             vmem(PARTIAL_SLOTS, cols, local, block, TILE, dtype=f32),
-            vmem(SLOTS, cols, local, block, TILE),
-            vmem(SLOTS, cols, local, block, TILE),
-            vmem(SLOTS, cols, local, block, TILE),
-            vmem(SLOTS, cols, local, block, TILE),
+            vmem(OUT_SLOTS, cols, local, block, TILE),
+            vmem(IN_SLOTS, cols, local, block, TILE),
+            vmem(OUT_SLOTS, cols, local, block, TILE),
+            vmem(IN_SLOTS, cols, local, block, TILE),
             vmem(SLOTS, 2, local, block, TILE),
             vmem(SLOTS, groups, local, block, TILE),
             vmem(GATHER_SLOTS, local, cols, block, TILE),
@@ -579,14 +627,17 @@
             vmem(PASSES, local, half, depth),
             sems(FRONT_SLOTS),
             sems(PASSES),
+            pltpu.SemaphoreType.DMA,
+            pltpu.SemaphoreType.DMA,
             sems(PASSES),
             sems(PASSES),
             sems(PASSES),
             sems(PASSES),
-            sems(SLOTS, cols),
-            sems(SLOTS, cols),
-            sems(SLOTS, cols),
-            sems(SLOTS, cols),
+            sems(PASSES),
+            sems(OUT_SLOTS, cols),
+            sems(IN_SLOTS, cols),
+            sems(OUT_SLOTS, cols),
+            sems(IN_SLOTS, cols),
             sems(SLOTS),
             sems(SLOTS),
             sems(SLOTS, groups),
@@ -599,11 +650,10 @@
         compiler_params=pltpu.CompilerParams(
             collective_id=0, has_side_effects=True, vmem_limit_bytes=67043328
         ),
-    )(first, fronts, second, row_keep.astype(f32), from_blocks, to_parents)
+    )(first, fronts, second, front_sizes, parent_ids, block_maps.T)
     sampled = sampled.transpose(1, 2, 0, 3).reshape(second_samples.shape)
     projected = projected.reshape(PASSES, local, half // block, block, depth)
     projected = projected.transpose(2, 0, 3, 1, 4).reshape(samples.shape)
-    projected = projected * col_keep[None].astype(projected.dtype)
     return sampled, projected
 
 

time: 263 us -> 228 us (0.87)
  Pallas kernels: 244 us -> 216 us
  other arithmetic: 6.68 us -> 0 us
    pallas_call x1, Pallas kernels: 244 us -> 216 us  [pipeline(): pl.pallas_call(functools.partial(fused, cols, groups), out_shape=(jax.Sha...]
    mul x2 -> x0, other arithmetic: 4.06 us -> none  [the longest x1 2.53 us: pipeline(): projected = projected * col_keep[None].astype(projected.dtype)]
    unnamed x12 -> x6, local copies, waits for them, and re-layouts: 6.18 us -> 5.91 us
where the time goes in v2:
time: 228 us
  Pallas kernels  216 us (95%)
  local copies, waits for them, and re-layouts  11.7 us (5%)
    pallas_call x1, Pallas kernels, pipeline(): pl.pallas_call(functools.partial(fused, cols, groups), out_shape=(jax.Sha...  216 us
    unnamed x6, local copies, waits for them, and re-layouts  5.91 us

profile of v2, /device:TPU:0, one launch (start us, length us, event | category | flops | bytes accessed | tf_op | source)
XLA Modules:
  0.0 227.9 jit_solution(11172458457524656770)
XLA Ops:
  0.6 0.0 copy-start
  0.6 3.0 %copy.8 = bf16[2,2,32,2,3072]{4,2,0,3,1:T(8,128)(2,1)} copy(bf16[2,2,32,2,3072]{4,3,2,1,0:T(2,128)(2,1)} %bitcast.17) | data formatting | bytes 3145728 | tf_op jit(solution)/shard_map/reshape | solution.py:591
  3.7 0.0 copy-done
  3.7 1.6 copy.9
  5.3 215.6 %shard_map.77 = (bf16[2,2,32,6144]{3,2,1,0:T(8,128)(2,1)}, bf16[2,2,64,3072]{3,2,1,0:T(8,128)(2,1)}) custom-call(bf16[2,2,64,3072]{3,2,1,0:T(8,128)(2,1)} %bitcast.15, bf16[2,6144,3072]{2,1,0:T(8,128)(2,1)} %fronts.1, bf16[2,2,32,6144]{3,2,1,0:T(8,128)(2,1)} %bitcast.16, s32[8]{0:T(128)} %sizes.1, s32[8]{0:T(128)} %parents.1, s32[2,8]{1,0:T(2,128)} %bitcast.21), custom_call_target="tpu_custom_call" | custom-call | tf_op jit(solution)/shard_map/pallas_call | solution.py:603
  220.9 0.0 copy-start.1
  220.9 4.3 %copy.11 = bf16[64,2,6144]{2,1,0:T(2,128)(2,1)} copy(bf16[64,2,6144]{2,0,1:T(8,128)(2,1)} %bitcast.20) | data formatting | bytes 3145728
  225.2 0.0 copy-done.1
  225.2 2.8 %copy.10 = bf16[2,2,32,2,3072]{4,3,2,1,0:T(2,128)(2,1)} copy(bf16[2,2,32,2,3072]{4,2,0,3,1:T(8,128)(2,1)S(1)} %bitcast.19) | data formatting | bytes 3145728 | tf_op jit(solution)/shard_map/transpose | solution.py:656
Async XLA Ops:
  0.6 3.0 %copy-start = (bf16[64,2,6144]{2,1,0:T(2,128)(2,1)S(1)}, bf16[64,2,6144]{2,1,0:T(2,128)(2,1)}, u32[]{:S(2)}) copy-start(bf16[64,2,6144]{2,1,0:T(2,128)(2,1)} %param.8) | copy-start | bytes 4718596
  220.9 4.3 %copy-start.1 = (bf16[2,2,64,3072]{3,2,1,0:T(8,128)(2,1)S(1)}, bf16[2,2,64,3072]{3,2,1,0:T(8,128)(2,1)}, u32[]{:S(2)}) copy-start(bf16[2,2,64,3072]{3,2,1,0:T(8,128)(2,1)} %get-tuple-element.5) | copy-start | bytes 4718596

commit v3 on v2

--- a/solution.py
+++ b/solution.py
@@ -7,20 +7,23 @@
 from jax.experimental.pallas import tpu as pltpu
 from jax.sharding import PartitionSpec as P
 
-PASSES = 2
+QUARTERS = 4
 TILE = 256
-BLOCK_TILES = 6
-HOP = 2
-ROUTE_LAG = 3 * HOP + 1
-COMBINE_LAG = ROUTE_LAG + 2
-SECOND_LAG = COMBINE_LAG + 3 * HOP
+EDGE_TILES = 8
+EARLY_QUARTERS = 2
+FIRST_PIECE = 3
+FINISH_LAG = 4
+ROUTE_LAG = 6
+COMBINE_LAG = 7
+FORWARD_LAGS = (9, 10)
+SECOND_LAG = 12
 SLOTS = 8
 OUT_SLOTS = 4
-IN_SLOTS = 10
+IN_SLOTS = 8
 GATHER_SLOTS = 12
-PARTIAL_SLOTS = 3 * HOP + 1
+PARTIAL_SLOTS = 17
 DRAIN = 2
-FRONT_SLOTS = 12
+FRONT_SLOTS = 13
 
 
 def swap_pairs(count):
@@ -118,8 +121,6 @@
     sampled_to,
     projected_to,
     second,
-    sampled,
-    projected,
     held,
     front_ring,
     partial,
@@ -131,7 +132,6 @@
     routed,
     gathered,
     total,
-    product_out,
     product_in,
     front_sem,
     local_sem,
@@ -158,13 +158,15 @@
     col = lax.axis_index("col")
     row = lax.axis_index("row")
     group = lax.axis_index("group")
-    passes, local, half, depth = samples.shape
-    block, tile = partial.shape[3:]
+    quarters, local, half, depth = samples.shape
+    block, tile = partial.shape[4:]
+    pieces = half // block
     height = fronts.shape[1]
     tiles = height // tile
-    steps = passes * tiles
+    steps = quarters * tiles // 2
     last = cols - 1
-    run = BLOCK_TILES
+    edge_steps = quarters * EDGE_TILES // 2
+    tail = steps - edge_steps
     other_row = 1 - row
 
     barrier = pltpu.get_barrier_semaphore()
@@ -186,10 +188,25 @@
     def _():
         greet({"col": col + 1})
 
-    def place(step):
-        begin = lax.div(step, passes * run)
-        rest = lax.rem(step, passes * run)
-        return lax.div(rest, run), begin * run + lax.rem(rest, run)
+    def narrow(step):
+        return (step < edge_steps) | (step >= tail)
+
+    def place(step, part):
+        within = jnp.where(step < edge_steps, step, step - tail)
+        first = jnp.where(step < edge_steps, 0, tiles - EDGE_TILES)
+        pairs = EDGE_TILES // 2
+        middle = jnp.maximum(step - edge_steps, 0)
+        edge = narrow(step)
+        within = jnp.where(edge, within, 0)
+        quarter = jnp.where(
+            edge, lax.div(within, pairs), 2 * lax.rem(middle, quarters // 2) + part
+        )
+        spot = jnp.where(
+            edge,
+            first + 2 * lax.rem(within, pairs) + part,
+            EDGE_TILES + lax.div(middle, quarters // 2),
+        )
+        return quarter, spot
 
     def lanes_of(spot):
         return pl.ds(pl.multiple_of(spot * tile, tile), tile)
@@ -213,28 +230,31 @@
         return at < own_sizes[front]
 
     second_copy = pltpu.make_async_copy(second_from, second, second_sem)
-    sampled_copy = pltpu.make_async_copy(sampled, sampled_to, sampled_sem)
 
     pl.semaphore_wait(barrier, groups + jnp.minimum(col, 1) + jnp.minimum(last - col, 1))
 
-    def own_half(turn):
-        return held.at[turn, :, pl.ds(pl.multiple_of(row * half, half), half), :]
-
-    def samples_copy(turn):
+    def samples_copy(quarter, front, piece):
+        at = pl.multiple_of(row * half + piece * block, block)
         return remote(
-            samples.at[turn],
-            own_half(turn),
-            samples_send.at[turn],
-            samples_recv.at[turn],
+            samples.at[quarter, front, pl.ds(piece * block, block), :],
+            held.at[quarter, front, pl.ds(at, block), :],
+            samples_send.at[quarter, front, piece],
+            samples_recv.at[quarter, front, piece],
             {"row": other_row},
         )
 
-    def samples_here(turn):
-        return pltpu.make_async_copy(samples.at[turn], own_half(turn), local_sem.at[turn])
-
-    for turn in range(passes):
-        samples_copy(turn).start()
-        samples_here(turn).start()
+    def samples_here(quarter):
+        ours = pl.ds(pl.multiple_of(row * half, half), half)
+        return pltpu.make_async_copy(
+            samples.at[quarter], held.at[quarter, :, ours, :], local_sem.at[quarter]
+        )
+
+    every_piece = [(front, piece) for front in range(local) for piece in range(pieces)]
+    for quarter in range(EARLY_QUARTERS):
+        for front, piece in every_piece:
+            samples_copy(quarter, front, piece).start()
+    for quarter in range(quarters):
+        samples_here(quarter).start()
     for spot in range(min(FRONT_SLOTS, tiles)):
         fetch(spot).start()
     second_copy.start()
@@ -309,32 +329,66 @@
     def first_product(step):
         @pl.when(live(step))
         def _():
-            turn, spot = place(step)
-
-            @pl.when(spot == 0)
-            def _():
-                samples_here(turn).wait()
-                samples_copy(turn).wait_recv()
+            spots = [place(step, part) for part in range(2)]
+            quarter, spot = spots[0]
+            size = cols * block
+
+            @pl.when((step < edge_steps) & (spot == 0))
+            def _():
+                samples_here(quarter).wait()
+                for front, piece in every_piece:
+                    samples_copy(quarter, front, piece).wait_recv()
                 for front in range(local):
-                    value = held[turn, front]
+                    value = held[quarter, front]
                     kept_here = kept(front, col * depth, value.shape)
-                    held[turn, front] = jnp.where(kept_here, value, jnp.zeros_like(value))
-
-            @pl.when(turn == 0)
+                    held[quarter, front] = jnp.where(kept_here, value, jnp.zeros_like(value))
+
+            @pl.when(quarter == 0)
             def _():
                 fetch(spot).wait()
 
-            slot = lax.rem(spot, FRONT_SLOTS)
-            into = lax.rem(step, PARTIAL_SLOTS)
-            for front in range(local):
-                value = lax.dot_general(
-                    held[turn, front],
-                    front_ring[slot, front],
+            def product(rows, spot, front):
+                return lax.dot_general(
+                    rows,
+                    front_ring[lax.rem(spot, FRONT_SLOTS), front],
                     (((1,), (1,)), ((), ())),
                     preferred_element_type=jnp.float32,
                 )
+
+            def keep(value, front, part, at):
+                into = lax.rem(at, PARTIAL_SLOTS)
                 for chunk in range(cols):
-                    partial[into, chunk, front] = value[chunk * block : (chunk + 1) * block]
+                    partial[into, chunk, front, part] = value[
+                        chunk * block : (chunk + 1) * block
+                    ].astype(partial.dtype)
+
+            def whole(front, spot):
+                rows = held[:, front].reshape(quarters * size, depth)
+                value = product(rows, spot, front)
+                return [value[quarter * size : (quarter + 1) * size] for quarter in range(quarters)]
+
+            @pl.when(narrow(step) & (quarter == 0))
+            def _():
+                fetch(spots[1][1]).wait()
+
+            @pl.when(step < edge_steps)
+            def _():
+                for front in range(local):
+                    for part, (_, tile_spot) in enumerate(spots):
+                        keep(product(held[quarter, front], tile_spot, front), front, part, step)
+
+            @pl.when((step >= tail) & (quarter == 0))
+            def _():
+                for front in range(local):
+                    for part, (_, tile_spot) in enumerate(spots):
+                        for index, value in enumerate(whole(front, tile_spot)):
+                            keep(value, front, part, step + index * (EDGE_TILES // 2))
+
+            @pl.when((step >= edge_steps) & (step < tail) & (quarter == 0))
+            def _():
+                for front in range(local):
+                    for index, value in enumerate(whole(front, spot)):
+                        keep(value, front, index % 2, step + index // 2)
 
     def hop(step, order, toward, edge, copy, out, received):
         @pl.when(spent(step))
@@ -361,55 +415,68 @@
                     def _():
                         copy(step, chunk).wait_recv()
                         out[slot, chunk] = (
-                            partial[own, chunk] + received[into, chunk].astype(jnp.float32)
+                            partial[own, chunk].astype(jnp.float32)
+                            + received[into, chunk].astype(jnp.float32)
                         ).astype(out.dtype)
 
                     copy(step, chunk).start()
+
+    def sampled_copies(step):
+        slot = lax.rem(step, SLOTS)
+        spots = [place(step, part) for part in range(2)]
+        return [
+            pltpu.make_async_copy(
+                across.at[slot, row, :, part],
+                sampled_to.at[:, quarter, :, lanes_of(spot)],
+                sampled_sem.at[slot, part],
+            )
+            for part, (quarter, spot) in enumerate(spots)
+        ]
 
     def finish(step):
         @pl.when(spent(step))
         def _():
             across_copy(step - DRAIN).wait_send()
+            for copy in sampled_copies(step - DRAIN):
+                copy.wait()
 
         @pl.when(live(step))
         def _():
             slot, into = lax.rem(step, SLOTS), lax.rem(step, IN_SLOTS)
             own = lax.rem(step, PARTIAL_SLOTS)
-            turn, spot = place(step)
-            lanes = lanes_of(spot)
+            spots = [place(step, part) for part in range(2)]
 
             def store(value):
                 for front in range(local):
-                    kept_here = kept(front, row * height + spot * tile, (block, tile))
-                    out = jnp.where(kept_here, value[front], 0.0).astype(sampled.dtype)
-                    sampled[front, turn, :, lanes] = out
-                    across[slot, row, front] = out
+                    for part, (quarter, spot) in enumerate(spots):
+                        kept_here = kept(front, row * height + spot * tile, (block, tile))
+                        out = jnp.where(kept_here, value[front, part], 0.0).astype(across.dtype)
+                        across[slot, row, front, part] = out
 
             @pl.when(col == 0)
             def _():
                 down_copy(step, col).wait_recv()
-                store(partial[own, col] + down_in[into, col].astype(jnp.float32))
+                store(partial[own, col].astype(jnp.float32) + down_in[into, col].astype(jnp.float32))
 
             @pl.when(col == last)
             def _():
                 up_copy(step, col).wait_recv()
-                store(partial[own, col] + up_in[into, col].astype(jnp.float32))
+                store(partial[own, col].astype(jnp.float32) + up_in[into, col].astype(jnp.float32))
 
             @pl.when((col > 0) & (col < last))
             def _():
                 up_copy(step, col).wait_recv()
                 down_copy(step, col).wait_recv()
                 store(
-                    partial[own, col]
+                    partial[own, col].astype(jnp.float32)
                     + up_in[into, col].astype(jnp.float32)
                     + down_in[into, col].astype(jnp.float32)
                 )
 
             across_copy(step).start()
 
-            @pl.when(step == steps - 1)
-            def _():
-                sampled_copy.start()
+            for copy in sampled_copies(step):
+                copy.start()
 
     def route(step):
         @pl.when(spent(step))
@@ -455,8 +522,8 @@
         @pl.when(live(step))
         def _():
             slot = lax.rem(step, SLOTS)
-            turn, spot = place(step)
-            lanes = lanes_of(spot)
+            spots = [place(step, part) for part in range(2)]
+
             @pl.when(step == 0)
             def _():
                 second_copy.wait()
@@ -469,13 +536,16 @@
                 for front in range(local)
             ]
             for parent in range(local):
-                value = second[parent, turn, :, lanes].astype(jnp.float32)
-                for child in range(number):
-                    value += weight(parents[child] == own_fronts[parent]) * parts[child]
-                value = jnp.where(
-                    kept(parent, row * height + spot * tile, value.shape), value, 0.0
-                )
-                gathered[lax.rem(step, GATHER_SLOTS), parent, col] = value.astype(gathered.dtype)
+                extension = weight(parents[0] == own_fronts[parent]) * parts[0]
+                for child in range(1, number):
+                    extension += weight(parents[child] == own_fronts[parent]) * parts[child]
+                for part, (quarter, spot) in enumerate(spots):
+                    value = second[parent, quarter, :, lanes_of(spot)].astype(jnp.float32)
+                    value += extension[part]
+                    kept_here = kept(parent, row * height + spot * tile, value.shape)
+                    gathered[lax.rem(step, GATHER_SLOTS), parent, col, part] = jnp.where(
+                        kept_here, value, 0.0
+                    ).astype(gathered.dtype)
             send_chunk(step, col)
 
     def forward(step, far):
@@ -503,14 +573,48 @@
                 below_copy(step, col + far).wait_recv()
                 below_copy(step, col + far).start()
 
-    def product_copy(turn):
+    def product_copy(quarter, front, piece):
+        rows = pl.ds(piece * block, block)
         return remote(
-            product_out.at[turn],
-            product_in.at[turn],
-            product_send.at[turn],
-            product_recv.at[turn],
+            held.at[quarter, front, rows, :],
+            product_in.at[quarter, front, rows, :],
+            product_send.at[quarter, front, piece],
+            product_recv.at[quarter, front, piece],
             {"row": other_row},
         )
+
+    def send_product(quarter, front, piece):
+        theirs = pl.ds(pl.multiple_of(other_row * half + piece * block, block), block)
+        held[quarter, front, pl.ds(piece * block, block), :] = total[
+            quarter, front, theirs, :
+        ].astype(held.dtype)
+        product_copy(quarter, front, piece).start()
+
+    def exchange(time):
+        late = len(every_piece) * (quarters - EARLY_QUARTERS)
+
+        @pl.when((time >= FIRST_PIECE) & (time < FIRST_PIECE + late))
+        def _():
+            number = time - FIRST_PIECE
+            quarter = EARLY_QUARTERS + lax.div(number, len(every_piece))
+            rest = lax.rem(number, len(every_piece))
+            for index, (front, piece) in enumerate(every_piece):
+
+                @pl.when(rest == index)
+                def _():
+                    samples_copy(quarter, front, piece).start()
+
+        done = time - SECOND_LAG - tail + 1 - EDGE_TILES // 2
+
+        @pl.when((done >= 0) & (done <= (quarters - 1) * len(every_piece)))
+        def _():
+            quarter = lax.div(done, len(every_piece))
+            rest = lax.rem(done, len(every_piece))
+            for index, (front, piece) in enumerate(every_piece):
+
+                @pl.when((rest == index) | (quarter == quarters - 1))
+                def _():
+                    send_product(quarter, front, piece)
 
     def second_product(step):
         @pl.when(live(step))
@@ -525,72 +629,124 @@
                 for chunk in range(1, cols):
                     below_copy(step, chunk).wait_recv()
 
-            turn, spot = place(step)
-            slot = lax.rem(spot, FRONT_SLOTS)
+            spots = [place(step, part) for part in range(2)]
+            quarter, spot = spots[0]
             from_slot = lax.rem(step, GATHER_SLOTS)
+            size = cols * block
             width = depth // 6 if depth % 768 == 0 else depth
-            for front in range(local):
-                rows = gathered[from_slot, front].reshape(cols * block, tile)
-                for begin in range(0, depth, width):
-                    total[turn, front, :, begin : begin + width] += jnp.dot(
-                        rows,
-                        front_ring[slot, front, :, begin : begin + width],
-                        preferred_element_type=jnp.float32,
-                    )
-
-            @pl.when(spot == tiles - 1)
-            def _():
-                theirs = pl.ds(pl.multiple_of(other_row * half, half), half)
+
+            def rows_of(front, part):
+                return gathered[from_slot, front, :, part].reshape(size, tile)
+
+            def product(rows, spot, front, begin):
+                return jnp.dot(
+                    rows,
+                    front_ring[lax.rem(spot, FRONT_SLOTS), front, :, begin : begin + width],
+                    preferred_element_type=jnp.float32,
+                )
+
+            @pl.when(narrow(step))
+            def _():
                 for front in range(local):
-                    product_out[turn, front] = total[turn, front, theirs].astype(
-                        product_out.dtype
-                    )
-                product_copy(turn).start()
-
-            @pl.when((turn == passes - 1) & (spot + FRONT_SLOTS < tiles))
-            def _():
-                fetch(spot + FRONT_SLOTS).start()
+                    rows = [rows_of(front, part) for part in range(2)]
+                    for begin in range(0, depth, width):
+                        total[quarter, front, :, begin : begin + width] += product(
+                            rows[0], spot, front, begin
+                        ) + product(rows[1], spots[1][1], front, begin)
+
+                @pl.when(quarter == quarters - 1)
+                def _():
+                    for _, done in spots:
+
+                        @pl.when(done + FRONT_SLOTS < tiles)
+                        def _():
+                            fetch(done + FRONT_SLOTS).start()
+
+            @pl.when(jnp.logical_not(narrow(step)))
+            def _():
+                for front in range(local):
+                    rows = jnp.concatenate([rows_of(front, part) for part in range(2)], axis=0)
+                    for begin in range(0, depth, width):
+                        value = product(rows, spot, front, begin)
+                        for part in range(2):
+                            total[quarter + part, front, :, begin : begin + width] += value[
+                                part * size : (part + 1) * size
+                            ]
+
+                @pl.when((quarter == quarters - 2) & (spot + FRONT_SLOTS < tiles))
+                def _():
+                    fetch(spot + FRONT_SLOTS).start()
+
+    odd = lax.rem(col, 2)
+
+    def up_hop(time):
+        hop(
+            time - lax.div(3 * col, 2),
+            range(cols - 1, 0, -1),
+            lambda chunk: chunk > col,
+            0,
+            up_copy,
+            up_out,
+            up_in,
+        )
+
+    def down_hop(time):
+        hop(
+            time - lax.div(3 * (last - col), 2),
+            range(last),
+            lambda chunk: chunk < col,
+            last,
+            down_copy,
+            down_out,
+            down_in,
+        )
 
     @pl.loop(0, steps + SECOND_LAG)
     def _(time):
         first_product(time)
-        hop(time - HOP * col, range(cols - 1, -1, -1), lambda chunk: chunk > col, 0, up_copy, up_out, up_in)
-        hop(time - HOP * (last - col), range(cols), lambda chunk: chunk < col, last, down_copy, down_out, down_in)
-        finish(time - HOP * last)
+        pl.when(odd == 0)(lambda: up_hop(time))
+        pl.when(odd == 1)(lambda: down_hop(time))
+        route(time - ROUTE_LAG)
+        forward(time - FORWARD_LAGS[0], 1)
         second_product(time - SECOND_LAG)
-        route(time - ROUTE_LAG)
+        pl.when(odd == 1)(lambda: up_hop(time))
+        pl.when(odd == 0)(lambda: down_hop(time))
+        finish(time - FINISH_LAG)
         combine(time - COMBINE_LAG)
-        for far in range(1, last):
-            forward(time - COMBINE_LAG - HOP * far, far)
-
-    def projected_copy(turn):
+        forward(time - FORWARD_LAGS[1], 2)
+        exchange(time)
+
+    def projected_copy(quarter):
         return pltpu.make_async_copy(
-            projected.at[turn], projected_to.at[turn], projected_sem.at[turn]
-        )
-
-    for turn in range(passes):
-        product_copy(turn).wait_recv()
+            product_in.at[quarter], projected_to.at[quarter], projected_sem.at[quarter]
+        )
+
+    for quarter in range(quarters):
         ours = pl.ds(pl.multiple_of(row * half, half), half)
         for front in range(local):
-            value = total[turn, front, ours] + product_in[turn, front].astype(jnp.float32)
+            for piece in range(pieces):
+                product_copy(quarter, front, piece).wait_recv()
+            value = total[quarter, front, ours] + product_in[quarter, front].astype(jnp.float32)
             kept_here = kept(front, col * depth, value.shape)
-            projected[turn, front] = jnp.where(kept_here, value, 0.0).astype(projected.dtype)
-        projected_copy(turn).start()
-    for turn in range(passes):
-        product_copy(turn).wait_send()
-        samples_copy(turn).wait_send()
-        projected_copy(turn).wait()
-    sampled_copy.wait()
+            product_in[quarter, front] = jnp.where(kept_here, value, 0.0).astype(
+                product_in.dtype
+            )
+        projected_copy(quarter).start()
+    for quarter in range(quarters):
+        for front, piece in every_piece:
+            product_copy(quarter, front, piece).wait_send()
+            samples_copy(quarter, front, piece).wait_send()
+        projected_copy(quarter).wait()
 
 
 def pipeline(fronts, samples, second_samples, front_sizes, parent_ids, block_maps):
     local, height, depth = fronts.shape
     groups, cols = lax.axis_size("group"), lax.axis_size("col")
-    block = second_samples.shape[0] // PASSES
-    half = samples.shape[0] // PASSES
-    first = samples.reshape(half // block, PASSES, block, local, depth)
-    first = first.transpose(1, 3, 0, 2, 4).reshape(PASSES, local, half, depth)
-    second = second_samples.reshape(PASSES, block, local, height).transpose(2, 0, 1, 3)
+    block = second_samples.shape[0] // QUARTERS
+    half = samples.shape[0] // QUARTERS
+    first = samples.reshape(half // block, QUARTERS, block, local, depth)
+    first = first.transpose(1, 3, 0, 2, 4).reshape(QUARTERS, local, half, depth)
+    second = second_samples.reshape(QUARTERS, block, local, height).transpose(2, 0, 1, 3)
     def vmem(*shape, dtype=jnp.bfloat16):
         return pltpu.VMEM(shape, dtype)
 
@@ -603,37 +759,34 @@
     sampled, projected = pl.pallas_call(
         functools.partial(fused, cols, groups),
         out_shape=(
-            jax.ShapeDtypeStruct((local, PASSES, block, height), jnp.bfloat16),
-            jax.ShapeDtypeStruct((PASSES, local, half, depth), jnp.bfloat16),
+            jax.ShapeDtypeStruct((local, QUARTERS, block, height), jnp.bfloat16),
+            jax.ShapeDtypeStruct((QUARTERS, local, half, depth), jnp.bfloat16),
         ),
         in_specs=[anywhere, anywhere, anywhere, in_smem, in_smem, in_smem],
         out_specs=(anywhere, anywhere),
         scratch_shapes=[
-            vmem(local, PASSES, block, height),
-            vmem(local, PASSES, block, height),
-            vmem(PASSES, local, half, depth),
-            vmem(PASSES, local, 2 * half, depth),
+            vmem(local, QUARTERS, block, height),
+            vmem(QUARTERS, local, 2 * half, depth),
             vmem(FRONT_SLOTS, local, TILE, depth),
-            vmem(PARTIAL_SLOTS, cols, local, block, TILE, dtype=f32),
-            vmem(OUT_SLOTS, cols, local, block, TILE),
-            vmem(IN_SLOTS, cols, local, block, TILE),
-            vmem(OUT_SLOTS, cols, local, block, TILE),
-            vmem(IN_SLOTS, cols, local, block, TILE),
-            vmem(SLOTS, 2, local, block, TILE),
-            vmem(SLOTS, groups, local, block, TILE),
-            vmem(GATHER_SLOTS, local, cols, block, TILE),
-            vmem(PASSES, local, 2 * half, depth, dtype=f32),
-            vmem(PASSES, local, half, depth),
-            vmem(PASSES, local, half, depth),
+            vmem(PARTIAL_SLOTS, cols, local, 2, block, TILE),
+            vmem(OUT_SLOTS, cols, local, 2, block, TILE),
+            vmem(IN_SLOTS, cols, local, 2, block, TILE),
+            vmem(OUT_SLOTS, cols, local, 2, block, TILE),
+            vmem(IN_SLOTS, cols, local, 2, block, TILE),
+            vmem(SLOTS, 2, local, 2, block, TILE),
+            vmem(SLOTS, groups, local, 2, block, TILE),
+            vmem(GATHER_SLOTS, local, cols, 2, block, TILE),
+            vmem(QUARTERS, local, 2 * half, depth, dtype=f32),
+            vmem(QUARTERS, local, half, depth),
             sems(FRONT_SLOTS),
-            sems(PASSES),
+            sems(QUARTERS),
             pltpu.SemaphoreType.DMA,
-            pltpu.SemaphoreType.DMA,
-            sems(PASSES),
-            sems(PASSES),
-            sems(PASSES),
-            sems(PASSES),
-            sems(PASSES),
+            sems(SLOTS, 2),
+            sems(QUARTERS),
+            sems(QUARTERS, local, half // block),
+            sems(QUARTERS, local, half // block),
+            sems(QUARTERS, local, half // block),
+            sems(QUARTERS, local, half // block),
             sems(OUT_SLOTS, cols),
             sems(IN_SLOTS, cols),
             sems(OUT_SLOTS, cols),
@@ -652,7 +805,7 @@
         ),
     )(first, fronts, second, front_sizes, parent_ids, block_maps.T)
     sampled = sampled.transpose(1, 2, 0, 3).reshape(second_samples.shape)
-    projected = projected.reshape(PASSES, local, half // block, block, depth)
+    projected = projected.reshape(QUARTERS, local, half // block, block, depth)
     projected = projected.transpose(2, 0, 3, 1, 4).reshape(samples.shape)
     return sampled, projected
 
@@ -660,14 +813,15 @@
 def fits(mesh, fronts, samples, second_samples, block_maps):
     rows, cols = mesh.shape["row"], mesh.shape["col"]
     height, depth = fronts.shape[1] // rows, fronts.shape[2] // cols
-    block = second_samples.shape[0] // cols // PASSES
+    block = second_samples.shape[0] // cols // QUARTERS
     return (
         rows == 2
         and cols == 4
         and block_maps.shape[1] == rows
         and height % TILE == 0
+        and height // TILE >= 2 * EDGE_TILES
         and depth % 128 == 0
-        and second_samples.shape[0] % (cols * PASSES) == 0
+        and second_samples.shape[0] % (cols * QUARTERS) == 0
         and block % 16 == 0
     )
 

time: 228 us -> 219 us (0.961)
  Pallas kernels: 216 us -> 207 us
    pallas_call x1, Pallas kernels: 216 us -> 207 us  [pipeline(): pl.pallas_call(functools.partial(fused, cols, groups), out_shape=(jax.Sha...]
where the time goes in v3:
time: 219 us
  Pallas kernels  207 us (95%)
  local copies, waits for them, and re-layouts  11.7 us (5%)
    pallas_call x1, Pallas kernels, pipeline(): pl.pallas_call(functools.partial(fused, cols, groups), out_shape=(jax.Sha...  207 us
    unnamed x6, local copies, waits for them, and re-layouts  5.91 us

profile of v3, /device:TPU:0, one launch (start us, length us, event | category | flops | bytes accessed | tf_op | source)
XLA Modules:
  0.0 219.1 jit_solution(3971222434376198561)
XLA Ops:
  0.6 0.0 copy-start
  0.6 3.0 %copy.8 = bf16[2,4,16,2,3072]{4,2,0,3,1:T(8,128)(2,1)} copy(bf16[2,4,16,2,3072]{4,3,2,1,0:T(2,128)(2,1)} %bitcast.17) | data formatting | bytes 3145728 | tf_op jit(solution)/shard_map/reshape | solution.py:747
  3.7 0.0 copy-done
  3.7 1.6 copy.9
  5.3 206.8 %shard_map.77 = (bf16[2,4,16,6144]{3,2,1,0:T(8,128)(2,1)}, bf16[4,2,32,3072]{3,2,1,0:T(8,128)(2,1)}) custom-call(bf16[4,2,32,3072]{3,2,1,0:T(8,128)(2,1)} %bitcast.15, bf16[2,6144,3072]{2,1,0:T(8,128)(2,1)} %fronts.1, bf16[2,4,16,6144]{3,2,1,0:T(8,128)(2,1)} %bitcast.16, s32[8]{0:T(128)} %sizes.1, s32[8]{0:T(128)} %parents.1, s32[2,8]{1,0:T(2,128)} %bitcast.21), custom_call_target="tpu_custom_call" | custom-call | tf_op jit(solution)/shard_map/pallas_call | solution.py:759
  212.1 0.0 copy-start.1
  212.1 4.3 %copy.11 = bf16[64,2,6144]{2,1,0:T(2,128)(2,1)} copy(bf16[64,2,6144]{2,0,1:T(8,128)(2,1)} %bitcast.20) | data formatting | bytes 3145728
  216.4 0.0 copy-done.1
  216.4 2.8 %copy.10 = bf16[2,4,16,2,3072]{4,3,2,1,0:T(2,128)(2,1)} copy(bf16[2,4,16,2,3072]{4,2,0,3,1:T(8,128)(2,1)S(1)} %bitcast.19) | data formatting | bytes 3145728 | tf_op jit(solution)/shard_map/transpose | solution.py:809
Async XLA Ops:
  0.6 3.0 %copy-start = (bf16[64,2,6144]{2,1,0:T(2,128)(2,1)S(1)}, bf16[64,2,6144]{2,1,0:T(2,128)(2,1)}, u32[]{:S(2)}) copy-start(bf16[64,2,6144]{2,1,0:T(2,128)(2,1)} %param.8) | copy-start | bytes 4718596
  212.1 4.3 %copy-start.1 = (bf16[4,2,32,3072]{3,2,1,0:T(8,128)(2,1)S(1)}, bf16[4,2,32,3072]{3,2,1,0:T(8,128)(2,1)}, u32[]{:S(2)}) copy-start(bf16[4,2,32,3072]{3,2,1,0:T(8,128)(2,1)} %get-tuple-element.5) | copy-start | bytes 4718596

commit v4 on v3

--- a/solution.py
+++ b/solution.py
@@ -11,7 +11,7 @@
 TILE = 256
 EDGE_TILES = 8
 EARLY_QUARTERS = 2
-FIRST_PIECE = 3
+FIRST_PIECE = 1
 FINISH_LAG = 4
 ROUTE_LAG = 6
 COMBINE_LAG = 7
@@ -21,8 +21,8 @@
 OUT_SLOTS = 4
 IN_SLOTS = 8
 GATHER_SLOTS = 12
-PARTIAL_SLOTS = 17
-DRAIN = 2
+PARTIAL_SLOTS = 18
+DRAIN = 3
 FRONT_SLOTS = 13
 
 
@@ -326,7 +326,7 @@
             {"col": jnp.maximum(col - 1, 0)},
         )
 
-    def first_product(step):
+    def first_product(step, front):
         @pl.when(live(step))
         def _():
             spots = [place(step, part) for part in range(2)]
@@ -335,19 +335,25 @@
 
             @pl.when((step < edge_steps) & (spot == 0))
             def _():
-                samples_here(quarter).wait()
-                for front, piece in every_piece:
+                if front == 0:
+                    samples_here(quarter).wait()
+                for piece in range(pieces):
                     samples_copy(quarter, front, piece).wait_recv()
-                for front in range(local):
-                    value = held[quarter, front]
-                    kept_here = kept(front, col * depth, value.shape)
-                    held[quarter, front] = jnp.where(kept_here, value, jnp.zeros_like(value))
-
-            @pl.when(quarter == 0)
-            def _():
-                fetch(spot).wait()
-
-            def product(rows, spot, front):
+                value = held[quarter, front]
+                kept_here = kept(front, col * depth, value.shape)
+                held[quarter, front] = jnp.where(kept_here, value, jnp.zeros_like(value))
+
+            if front == 0:
+
+                @pl.when(quarter == 0)
+                def _():
+                    fetch(spot).wait()
+
+                @pl.when(narrow(step) & (quarter == 0))
+                def _():
+                    fetch(spots[1][1]).wait()
+
+            def product(rows, spot):
                 return lax.dot_general(
                     rows,
                     front_ring[lax.rem(spot, FRONT_SLOTS), front],
@@ -355,40 +361,33 @@
                     preferred_element_type=jnp.float32,
                 )
 
-            def keep(value, front, part, at):
+            def keep(value, part, at):
                 into = lax.rem(at, PARTIAL_SLOTS)
                 for chunk in range(cols):
                     partial[into, chunk, front, part] = value[
                         chunk * block : (chunk + 1) * block
                     ].astype(partial.dtype)
 
-            def whole(front, spot):
+            def whole(spot):
                 rows = held[:, front].reshape(quarters * size, depth)
-                value = product(rows, spot, front)
+                value = product(rows, spot)
                 return [value[quarter * size : (quarter + 1) * size] for quarter in range(quarters)]
 
-            @pl.when(narrow(step) & (quarter == 0))
-            def _():
-                fetch(spots[1][1]).wait()
-
             @pl.when(step < edge_steps)
             def _():
-                for front in range(local):
-                    for part, (_, tile_spot) in enumerate(spots):
-                        keep(product(held[quarter, front], tile_spot, front), front, part, step)
+                for part, (_, tile_spot) in enumerate(spots):
+                    keep(product(held[quarter, front], tile_spot), part, step)
 
             @pl.when((step >= tail) & (quarter == 0))
             def _():
-                for front in range(local):
-                    for part, (_, tile_spot) in enumerate(spots):
-                        for index, value in enumerate(whole(front, tile_spot)):
-                            keep(value, front, part, step + index * (EDGE_TILES // 2))
+                for part, (_, tile_spot) in enumerate(spots):
+                    for index, value in enumerate(whole(tile_spot)):
+                        keep(value, part, step + index * (EDGE_TILES // 2))
 
             @pl.when((step >= edge_steps) & (step < tail) & (quarter == 0))
             def _():
-                for front in range(local):
-                    for index, value in enumerate(whole(front, spot)):
-                        keep(value, front, index % 2, step + index // 2)
+                for index, value in enumerate(whole(spot)):
+                    keep(value, index % 2, step + index // 2)
 
     def hop(step, order, toward, edge, copy, out, received):
         @pl.when(spent(step))
@@ -616,18 +615,20 @@
                 def _():
                     send_product(quarter, front, piece)
 
-    def second_product(step):
+    def second_product(step, front):
         @pl.when(live(step))
         def _():
-            @pl.when(col == last)
-            def _():
-                for chunk in range(last):
-                    above_copy(step, chunk).wait_recv()
-
-            @pl.when(col == 0)
-            def _():
-                for chunk in range(1, cols):
-                    below_copy(step, chunk).wait_recv()
+            if front == 0:
+
+                @pl.when(col == last)
+                def _():
+                    for chunk in range(last):
+                        above_copy(step, chunk).wait_recv()
+
+                @pl.when(col == 0)
+                def _():
+                    for chunk in range(1, cols):
+                        below_copy(step, chunk).wait_recv()
 
             spots = [place(step, part) for part in range(2)]
             quarter, spot = spots[0]
@@ -635,10 +636,10 @@
             size = cols * block
             width = depth // 6 if depth % 768 == 0 else depth
 
-            def rows_of(front, part):
+            def rows_of(part):
                 return gathered[from_slot, front, :, part].reshape(size, tile)
 
-            def product(rows, spot, front, begin):
+            def product(rows, spot, begin):
                 return jnp.dot(
                     rows,
                     front_ring[lax.rem(spot, FRONT_SLOTS), front, :, begin : begin + width],
@@ -647,35 +648,37 @@
 
             @pl.when(narrow(step))
             def _():
-                for front in range(local):
-                    rows = [rows_of(front, part) for part in range(2)]
-                    for begin in range(0, depth, width):
-                        total[quarter, front, :, begin : begin + width] += product(
-                            rows[0], spot, front, begin
-                        ) + product(rows[1], spots[1][1], front, begin)
-
-                @pl.when(quarter == quarters - 1)
-                def _():
-                    for _, done in spots:
-
-                        @pl.when(done + FRONT_SLOTS < tiles)
-                        def _():
-                            fetch(done + FRONT_SLOTS).start()
+                rows = [rows_of(part) for part in range(2)]
+                for begin in range(0, depth, width):
+                    total[quarter, front, :, begin : begin + width] += product(
+                        rows[0], spot, begin
+                    ) + product(rows[1], spots[1][1], begin)
+
+                if front == local - 1:
+
+                    @pl.when(quarter == quarters - 1)
+                    def _():
+                        for _, done in spots:
+
+                            @pl.when(done + FRONT_SLOTS < tiles)
+                            def _():
+                                fetch(done + FRONT_SLOTS).start()
 
             @pl.when(jnp.logical_not(narrow(step)))
             def _():
-                for front in range(local):
-                    rows = jnp.concatenate([rows_of(front, part) for part in range(2)], axis=0)
-                    for begin in range(0, depth, width):
-                        value = product(rows, spot, front, begin)
-                        for part in range(2):
-                            total[quarter + part, front, :, begin : begin + width] += value[
-                                part * size : (part + 1) * size
-                            ]
-
-                @pl.when((quarter == quarters - 2) & (spot + FRONT_SLOTS < tiles))
-                def _():
-                    fetch(spot + FRONT_SLOTS).start()
+                rows = jnp.concatenate([rows_of(part) for part in range(2)], axis=0)
+                for begin in range(0, depth, width):
+                    value = product(rows, spot, begin)
+                    for part in range(2):
+                        total[quarter + part, front, :, begin : begin + width] += value[
+                            part * size : (part + 1) * size
+                        ]
+
+                if front == local - 1:
+
+                    @pl.when((quarter == quarters - 2) & (spot + FRONT_SLOTS < tiles))
+                    def _():
+                        fetch(spot + FRONT_SLOTS).start()
 
     odd = lax.rem(col, 2)
 
@@ -701,19 +704,25 @@
             down_in,
         )
 
-    @pl.loop(0, steps + SECOND_LAG)
+    first_product(jnp.int32(0), 0)
+
+    @pl.loop(0, steps + max(SECOND_LAG, FORWARD_LAGS[1] + DRAIN))
     def _(time):
-        first_product(time)
+        for front in range(1, local):
+            first_product(time, front)
         pl.when(odd == 0)(lambda: up_hop(time))
         pl.when(odd == 1)(lambda: down_hop(time))
+        forward(time - FORWARD_LAGS[0], 1)
         route(time - ROUTE_LAG)
-        forward(time - FORWARD_LAGS[0], 1)
-        second_product(time - SECOND_LAG)
+        second_product(time - SECOND_LAG, 0)
+        first_product(time + 1, 0)
+        combine(time - COMBINE_LAG)
+        forward(time - FORWARD_LAGS[1], 2)
         pl.when(odd == 1)(lambda: up_hop(time))
         pl.when(odd == 0)(lambda: down_hop(time))
         finish(time - FINISH_LAG)
-        combine(time - COMBINE_LAG)
-        forward(time - FORWARD_LAGS[1], 2)
+        for front in range(1, local):
+            second_product(time - SECOND_LAG, front)
         exchange(time)
 
     def projected_copy(quarter):

time: 219 us -> 212 us (0.968)
  Pallas kernels: 207 us -> 199 us
    pallas_call x1, Pallas kernels: 207 us -> 199 us  [pipeline(): pl.pallas_call(functools.partial(fused, cols, groups), out_shape=(jax.Sha...]
where the time goes in v4:
time: 212 us; the launch traced here: 211 us
  Pallas kernels  199 us (94%)
  local copies, waits for them, and re-layouts  11.7 us (6%)
    pallas_call x1, Pallas kernels, pipeline(): pl.pallas_call(functools.partial(fused, cols, groups), out_shape=(jax.Sha...  199 us
    unnamed x6, local copies, waits for them, and re-layouts  5.91 us

profile of v4, /device:TPU:0, one launch (start us, length us, event | category | flops | bytes accessed | tf_op | source)
XLA Modules:
  0.0 211.4 jit_solution(13061791437383612322)
XLA Ops:
  0.6 0.0 copy-start
  0.6 3.0 %copy.8 = bf16[2,4,16,2,3072]{4,2,0,3,1:T(8,128)(2,1)} copy(bf16[2,4,16,2,3072]{4,3,2,1,0:T(2,128)(2,1)} %bitcast.17) | data formatting | bytes 3145728 | tf_op jit(solution)/shard_map/reshape | solution.py:756
  3.7 0.0 copy-done
  3.7 1.6 copy.9
  5.3 199.1 %shard_map.77 = (bf16[2,4,16,6144]{3,2,1,0:T(8,128)(2,1)}, bf16[4,2,32,3072]{3,2,1,0:T(8,128)(2,1)}) custom-call(bf16[4,2,32,3072]{3,2,1,0:T(8,128)(2,1)} %bitcast.15, bf16[2,6144,3072]{2,1,0:T(8,128)(2,1)} %fronts.1, bf16[2,4,16,6144]{3,2,1,0:T(8,128)(2,1)} %bitcast.16, s32[8]{0:T(128)} %sizes.1, s32[8]{0:T(128)} %parents.1, s32[2,8]{1,0:T(2,128)} %bitcast.21), custom_call_target="tpu_custom_call" | custom-call | tf_op jit(solution)/shard_map/pallas_call | solution.py:768
  204.3 0.0 copy-start.1
  204.4 4.3 %copy.11 = bf16[64,2,6144]{2,1,0:T(2,128)(2,1)} copy(bf16[64,2,6144]{2,0,1:T(8,128)(2,1)} %bitcast.20) | data formatting | bytes 3145728
  208.6 0.0 copy-done.1
  208.6 2.8 %copy.10 = bf16[2,4,16,2,3072]{4,3,2,1,0:T(2,128)(2,1)} copy(bf16[2,4,16,2,3072]{4,2,0,3,1:T(8,128)(2,1)S(1)} %bitcast.19) | data formatting | bytes 3145728 | tf_op jit(solution)/shard_map/transpose | solution.py:818
Async XLA Ops:
  0.6 3.0 %copy-start = (bf16[64,2,6144]{2,1,0:T(2,128)(2,1)S(1)}, bf16[64,2,6144]{2,1,0:T(2,128)(2,1)}, u32[]{:S(2)}) copy-start(bf16[64,2,6144]{2,1,0:T(2,128)(2,1)} %param.8) | copy-start | bytes 4718596
  204.3 4.3 %copy-start.1 = (bf16[4,2,32,3072]{3,2,1,0:T(8,128)(2,1)S(1)}, bf16[4,2,32,3072]{3,2,1,0:T(8,128)(2,1)}, u32[]{:S(2)}) copy-start(bf16[4,2,32,3072]{3,2,1,0:T(8,128)(2,1)} %get-tuple-element.5) | copy-start | bytes 4718596

commit v5 on v4

--- a/solution.py
+++ b/solution.py
@@ -11,7 +11,7 @@
 TILE = 256
 EDGE_TILES = 8
 EARLY_QUARTERS = 2
-FIRST_PIECE = 1
+FIRST_PIECE = 2
 FINISH_LAG = 4
 ROUTE_LAG = 6
 COMBINE_LAG = 7

time: 212 us -> 212 us (level)
  no operation moved by 1% of the time
where the time goes in v5:
time: 212 us; the launch traced here: 211 us
  Pallas kernels  199 us (94%)
  local copies, waits for them, and re-layouts  11.7 us (6%)
    pallas_call x1, Pallas kernels, pipeline(): pl.pallas_call(functools.partial(fused, cols, groups), out_shape=(jax.Sha...  199 us
    unnamed x6, local copies, waits for them, and re-layouts  5.91 us

profile of v5, /device:TPU:0, one launch (start us, length us, event | category | flops | bytes accessed | tf_op | source)
XLA Modules:
  0.0 211.4 jit_solution(2344471206073889244)
XLA Ops:
  0.6 0.0 copy-start
  0.6 3.0 %copy.8 = bf16[2,4,16,2,3072]{4,2,0,3,1:T(8,128)(2,1)} copy(bf16[2,4,16,2,3072]{4,3,2,1,0:T(2,128)(2,1)} %bitcast.17) | data formatting | bytes 3145728 | tf_op jit(solution)/shard_map/reshape | solution.py:756
  3.7 0.0 copy-done
  3.7 1.6 copy.9
  5.3 199.1 %shard_map.77 = (bf16[2,4,16,6144]{3,2,1,0:T(8,128)(2,1)}, bf16[4,2,32,3072]{3,2,1,0:T(8,128)(2,1)}) custom-call(bf16[4,2,32,3072]{3,2,1,0:T(8,128)(2,1)} %bitcast.15, bf16[2,6144,3072]{2,1,0:T(8,128)(2,1)} %fronts.1, bf16[2,4,16,6144]{3,2,1,0:T(8,128)(2,1)} %bitcast.16, s32[8]{0:T(128)} %sizes.1, s32[8]{0:T(128)} %parents.1, s32[2,8]{1,0:T(2,128)} %bitcast.21), custom_call_target="tpu_custom_call" | custom-call | tf_op jit(solution)/shard_map/pallas_call | solution.py:768
  204.4 0.0 copy-start.1
  204.4 4.3 %copy.11 = bf16[64,2,6144]{2,1,0:T(2,128)(2,1)} copy(bf16[64,2,6144]{2,0,1:T(8,128)(2,1)} %bitcast.20) | data formatting | bytes 3145728
  208.7 0.0 copy-done.1
  208.7 2.8 %copy.10 = bf16[2,4,16,2,3072]{4,3,2,1,0:T(2,128)(2,1)} copy(bf16[2,4,16,2,3072]{4,2,0,3,1:T(8,128)(2,1)S(1)} %bitcast.19) | data formatting | bytes 3145728 | tf_op jit(solution)/shard_map/transpose | solution.py:818
Async XLA Ops:
  0.6 3.0 %copy-start = (bf16[64,2,6144]{2,1,0:T(2,128)(2,1)S(1)}, bf16[64,2,6144]{2,1,0:T(2,128)(2,1)}, u32[]{:S(2)}) copy-start(bf16[64,2,6144]{2,1,0:T(2,128)(2,1)} %param.8) | copy-start | bytes 4718596
  204.4 4.3 %copy-start.1 = (bf16[4,2,32,3072]{3,2,1,0:T(8,128)(2,1)S(1)}, bf16[4,2,32,3072]{3,2,1,0:T(8,128)(2,1)}, u32[]{:S(2)}) copy-start(bf16[4,2,32,3072]{3,2,1,0:T(8,128)(2,1)} %get-tuple-element.5) | copy-start | bytes 4718596
